TPU v7x, 32 devices: a whole 2x2x4 slice. The times are simulated.
32 devices in a mesh: dp: 2 (over x), cp: 4 (over z), tp: 4 (over y, core).
Axes of the slice: x: 2, y: 2, z: 4, core: 2. Of those that a mesh axis runs over, the one named last changes fastest.
Arguments:
- x_tok: bfloat16 [16384, 1024], P(('dp', 'cp', 'tp')), parts along dimension 0
- w_q: bfloat16 [1024, 32, 32], P(None, 'tp')
- w_k: bfloat16 [1024, 8, 32], P(None, 'tp')
- w_v: bfloat16 [1024, 8, 32], P(None, 'tp')
- w_o: bfloat16 [32, 32, 1024], P('tp')
- expert_ids: int32 [16384, 2], P(('dp', 'cp', 'tp')), parts along dimension 0
- gate_wts: float32 [16384, 2], P(('dp', 'cp', 'tp')), parts along dimension 0
- w_gate: bfloat16 [16, 1024, 1792], P(('cp', 'tp'))
- w_up: bfloat16 [16, 1024, 1792], P(('cp', 'tp'))
- w_down: bfloat16 [16, 1792, 1024], P(('cp', 'tp'))
Outputs:
- output: bfloat16 [16384, 1024], P(('dp', 'cp', 'tp')), parts along dimension 0
There are 2 independent parts. A program takes and returns all parts, laid end to end along the dimension named above; an argument that names none is the same for every part.
All inputs are finite; a program needn't handle non-finite values.
Results may differ from a plain program's by a relative error of at most 0.0113248.
Values are sent between devices in bfloat16 or wider.
A program may use at most 1 GiB of HBM per device.

v0:
```python
import jax
import jax.numpy as jnp
from jax import lax
from jax.sharding import PartitionSpec as P


def seq_positions(cp_index, n_cp, half_len):
    chunk_len = half_len // 2
    in_half = jnp.arange(half_len)
    return jnp.where(in_half < chunk_len, cp_index * chunk_len + in_half, (2 * n_cp - 1 - cp_index) * chunk_len + in_half - chunk_len)


def attend_block(q_loc, k_blk, v_blk, q_pos, k_pos, run_max, run_sum, run_acc):
    head_dim = q_loc.shape[-1]
    scores = jnp.einsum("qgrd,kgd->grqk", q_loc, k_blk, preferred_element_type=jnp.float32) * (head_dim ** -0.5)
    allowed = q_pos[:, None] >= k_pos[None, :]
    scores = jnp.where(allowed, scores, -1e30)
    new_max = jnp.maximum(run_max, jnp.max(scores, axis=-1))
    prob_vals = jnp.exp(scores - new_max[..., None])
    rescale = jnp.exp(run_max - new_max)
    new_sum = run_sum * rescale + jnp.sum(prob_vals, axis=-1)
    new_acc = run_acc * rescale[..., None] + jnp.einsum("grqk,kgd->grqd", prob_vals.astype(jnp.bfloat16), v_blk, preferred_element_type=jnp.float32)
    return new_max, new_sum, new_acc


def solution(mesh):
    n_cp = mesh.shape["cp"]
    n_tp = mesh.shape["tp"]
    row_spec = P(("dp", "cp", "tp"), None)
    head_spec = P(None, "tp", None)
    expert_spec = P(("cp", "tp"), None, None)

    def device_step(x_loc, w_q, w_k, w_v, w_o, ids_loc, gates_loc, w_gate, w_up, w_down):
        tok_dev, hid_dim = x_loc.shape
        top_k = ids_loc.shape[1]
        kv_loc = w_k.shape[1]
        head_dim = w_q.shape[2]
        grp_size = w_q.shape[1] // kv_loc
        local_exp = w_gate.shape[0]
        n_experts = local_exp * n_cp * n_tp // 2
        capacity = top_k * tok_dev // n_experts
        half_hid = hid_dim // 2
        cp_index = lax.axis_index("cp")
        tp_index = lax.axis_index("tp")

        x_half = lax.all_gather(x_loc, "tp", axis=0, tiled=True)
        half_len = x_half.shape[0]
        q_loc = jnp.einsum("sh,hnd->snd", x_half, w_q, preferred_element_type=jnp.float32).astype(jnp.bfloat16).reshape(half_len, kv_loc, grp_size, head_dim)
        k_cur = jnp.einsum("sh,hnd->snd", x_half, w_k, preferred_element_type=jnp.float32).astype(jnp.bfloat16)
        v_cur = jnp.einsum("sh,hnd->snd", x_half, w_v, preferred_element_type=jnp.float32).astype(jnp.bfloat16)
        q_pos = seq_positions(cp_index, n_cp, half_len)
        init_max = jnp.full((kv_loc, grp_size, half_len), -1e30, jnp.float32)
        init_sum = jnp.zeros((kv_loc, grp_size, half_len), jnp.float32)
        init_acc = jnp.zeros((kv_loc, grp_size, half_len, head_dim), jnp.float32)
        first_state = attend_block(q_loc, k_cur, v_cur, q_pos, q_pos, init_max, init_sum, init_acc)
        shift_perm = [(src_dev, (src_dev + 1) % n_cp) for src_dev in range(n_cp)]

        def kv_step(step_idx, kv_state):
            k_blk, v_blk, cur_max, cur_sum, cur_acc = kv_state
            k_blk = lax.ppermute(k_blk, "cp", shift_perm)
            v_blk = lax.ppermute(v_blk, "cp", shift_perm)
            k_pos = seq_positions((cp_index - step_idx) % n_cp, n_cp, half_len)
            cur_max, cur_sum, cur_acc = attend_block(q_loc, k_blk, v_blk, q_pos, k_pos, cur_max, cur_sum, cur_acc)
            return k_blk, v_blk, cur_max, cur_sum, cur_acc

        kv_state = lax.fori_loop(1, n_cp, kv_step, (k_cur, v_cur) + first_state)
        attn_out = (kv_state[4] / kv_state[3][..., None]).astype(jnp.bfloat16)
        w_o_view = w_o.reshape(kv_loc, grp_size, head_dim, hid_dim)
        attn_part = jnp.einsum("grqd,grdh->qh", attn_out, w_o_view, preferred_element_type=jnp.float32)
        attn_rows = lax.psum_scatter(attn_part, "tp", scatter_dimension=0, tiled=True)
        h_loc = (x_loc.astype(jnp.float32) + attn_rows).astype(jnp.bfloat16)

        flat_ids = ids_loc.reshape(-1)
        one_hot = (flat_ids[:, None] == jnp.arange(n_experts)[None, :]).astype(jnp.int32)
        slot_ids = jnp.sum(jnp.cumsum(one_hot, axis=0) * one_hot, axis=1) - 1
        dest_idx = flat_ids * capacity + slot_ids
        choice_rows = jnp.arange(tok_dev * top_k, dtype=jnp.int32) // top_k
        slot_rows = jax.ops.segment_sum(choice_rows, dest_idx, num_segments=n_experts * capacity)
        send_buf = jnp.take(h_loc, slot_rows, axis=0).reshape(n_cp, n_tp // 2, 1, local_exp, capacity, hid_dim)
        send_buf = jnp.broadcast_to(send_buf, (n_cp, n_tp // 2, 2, local_exp, capacity, hid_dim)).reshape(n_cp, n_tp, local_exp, capacity, hid_dim)
        recv_buf = lax.all_to_all(send_buf, "tp", 1, 1, tiled=True)
        recv_buf = lax.all_to_all(recv_buf, "cp", 0, 0, tiled=True)

        gate_pre = jnp.einsum("uvech,ehf->uvecf", recv_buf, w_gate, preferred_element_type=jnp.float32)
        up_pre = jnp.einsum("uvech,ehf->uvecf", recv_buf, w_up, preferred_element_type=jnp.float32)
        hidden = (jax.nn.silu(gate_pre) * up_pre).astype(jnp.bfloat16)
        z_part = jnp.einsum("uvecf,efh->uvech", hidden, w_down, preferred_element_type=jnp.float32)

        my_half = tp_index % 2
        keep_part = lax.dynamic_slice_in_dim(z_part, my_half * half_hid, half_hid, axis=4)
        send_part = lax.dynamic_slice_in_dim(z_part, (1 - my_half) * half_hid, half_hid, axis=4)
        pair_perm = [(dev_idx, dev_idx ^ 1) for dev_idx in range(n_tp)]
        z_half = (keep_part + lax.ppermute(send_part, "tp", pair_perm)).astype(jnp.bfloat16)

        back_buf = lax.all_to_all(z_half, "cp", 0, 0, tiled=True)
        back_buf = lax.all_to_all(back_buf, "tp", 1, 1, tiled=True)
        z_full = back_buf.reshape(n_cp, n_tp // 2, 2, local_exp, capacity, half_hid).transpose(0, 1, 3, 4, 2, 5).reshape(n_experts * capacity, hid_dim)
        picked = jnp.take(z_full, dest_idx, axis=0).reshape(tok_dev, top_k, hid_dim)
        y_loc = h_loc.astype(jnp.float32) + jnp.sum(gates_loc[:, :, None] * picked, axis=1)
        return y_loc.astype(jnp.bfloat16)

    return jax.shard_map(device_step, mesh=mesh, in_specs=(row_spec, head_spec, head_spec, head_spec, P("tp", None, None), row_spec, row_spec, expert_spec, expert_spec, expert_spec), out_specs=row_spec, check_vma=False)
```

profile of v0, /device:TPU:0, one launch (start us, length us, event | category | flops | bytes accessed | tf_op | source)
XLA Modules:
  0.0 1043.7 jit_solution(10124679814584178241)
XLA Ops:
  6.5 0.7 all-gather.2.cloned.1.call-update
  7.3 4.2 broadcast_compare_fusion.1
  11.5 34.5 %all-gather.2.cloned.1.call-done = bf16[2048,1024]{1,0:T(8,128)(2,1)} async-done(((bf16[512,1024]{1,0:T(8,128)(2,1)}), bf16[2048,1024]{1,0:T(8,128)(2,1)}) %all-gather.2.cloned.1.call-update) | async-done | bytes 4194320 | tf_op jit(solution)/shard_map/all_gather | solution.py:46
  46.0 3.6 bitcast_convert_fusion
  49.6 1.4 bitcast_convert_fusion.1
  51.0 0.8 copy-done.3
  51.8 44.2 %fusion.18 = (f32[2,4,2048]{2,1,0:T(4,128)S(1)}, f32[2,2048,2048,4]{2,1,3,0:T(8,128)}) fusion(pred[2048,2048]{0,1:T(8,128)(4,1)S(1)} %copy-done.3, bf16[2048,2,4,32]{0,3,2,1:T(8,128)(2,1)S(1)} %bitcast.234, bf16[2048,2,32]{0,2,1:T(8,128)(2,1)S(1)} %bitcast_convert_fusion.1), kind=kOutput, calls=%fused_computation.27 | convolution fusion | flops 2248130560 | bytes 139788288 | tf_op jit(solution)/shard_map/qgrd,kgd->grqk/dot_general | solution.py:15
  96.0 0.6 broadcast_maximum_fusion
  96.6 42.6 %fusion.17 = f32[2,4,2048]{2,1,0:T(4,128)S(1)} fusion(f32[2,2048,2048,4]{2,1,3,0:T(8,128)} %get-tuple-element.285, f32[2,4,2048]{2,1,0:T(4,128)} %broadcast_maximum_fusion, pred[2048,2048]{0,1:T(8,128)(4,1)} %broadcast_compare_fusion.1), kind=kLoop, calls=%fused_computation.26 | loop fusion | flops 134201344 | bytes 138543104 | tf_op jit(solution)/shard_map/reduce_sum | solution.py:21
  139.3 3.7 fusion.63
  143.1 47.1 %broadcast_add_fusion = f32[2,4,2048,32]{2,3,1,0:T(8,128)} fusion(f32[2,4,2048]{2,1,0:T(4,128)S(1)} %get-tuple-element.282, f32[2,2048,2048,4]{2,1,3,0:T(8,128)} %get-tuple-element.285, f32[2,4,2048]{2,1,0:T(4,128)} %broadcast_maximum_fusion, pred[2048,2048]{0,1:T(8,128)(4,1)S(1)} %copy-done.4, bf16[2048,2,32]{0,2,1:T(8,128)(2,1)S(1)} %convert_element_type.53), kind=kOutput, calls=%fused_computation.59 | convolution fusion | flops 2282225664 | bytes 140902400 | tf_op jit(solution)/shard_map/grqk,kgd->grqd/dot_general | solution.py:22
  190.2 441.8 %while.24 = (s32[]{:T(128)}, bf16[2048,2,32]{0,2,1:T(8,128)(2,1)S(1)}, bf16[2048,2,32]{0,2,1:T(8,128)(2,1)S(1)}, f32[2,4,2048]{2,1,0:T(4,128)}, f32[2,4,2048]{2,...) while((s32[]{:T(128)}, ...), condition=%wide.region_5.6_spmd.clone, body=%wide.region_2.5_spmd.clone.sunk | while | flops 4669360128 | bytes 446202272 | solution.py:66
  190.2 1.5 collective-permute-start
  191.7 1.5 collective-permute-start.1
  193.2 2.9 broadcast_compare_fusion.3
  196.1 5.1 collective-permute-done
  201.2 44.2 %fusion.90 = (f32[2,4,2048]{2,1,0:T(4,128)S(1)}, f32[2,2048,2048,4]{2,1,3,0:T(8,128)}) fusion(pred[2048,2048]{0,1:T(8,128)(4,1)S(1)} %broadcast_compare_fusion.3, bf16[2048,2,4,32]{0,3,2,1:T(8,128)(2,1)S(1)} %get-tuple-element.402, bf16[2048,2,32]{0,2,1:T(8,128)(2,1)S(1)} %collective-permute-done), kind=kOutput, calls=%fused_computation.8.clone.1 | convolution fusion | flops 2248130560 | bytes 139788288 | tf_op jit(solution)/shard_map/while/body/eval_jaxpr/qgrd,kgd->grqk/dot_general | solution.py:15
  245.4 0.9 max.12
  246.3 42.4 %fusion.91 = f32[2,4,2048]{2,1,0:T(4,128)S(1)} fusion(f32[2,2048,2048,4]{2,1,3,0:T(8,128)} %get-tuple-element.360, f32[2,4,2048]{2,1,0:T(4,128)S(1)} %max.12, pred[2048,2048]{0,1:T(8,128)(4,1)} %copy-done.1), kind=kLoop, calls=%fused_computation.7.clone.1 | loop fusion | flops 134201344 | bytes 138543104 | tf_op jit(solution)/shard_map/while/body/eval_jaxpr/reduce_sum | solution.py:21
  288.7 0.9 multiply_add_fusion.4
  289.6 0.6 copy.75
  290.3 47.9 %multiply_add_fusion.5 = f32[2,4,2048,32]{2,3,1,0:T(8,128)} fusion(f32[2,4,2048,32]{2,3,1,0:T(8,128)} %get-tuple-element.384, f32[2,4,2048]{2,1,0:T(4,128)S(1)} %bitcast.226, f32[2,2048,2048,4]{2,1,3,0:T(8,128)} %get-tuple-element.360, f32[2,4,2048]{2,1,0:T(4,128)S(1)} %max.12, pred[2048,2048]{0,1:T(8,128)(4,1)} %copy-done.1, ...), kind=kOutput, calls=%fused_computation.12.clone.1 | convolution fusion | flops 2282749952 | bytes 142999552 | tf_op jit(solution)/shard_map/while/body/eval_jaxpr/grqk,kgd->grqd/dot_general | solution.py:22
  338.2 1.2 collective-permute-start.1
  339.4 2.9 broadcast_compare_fusion.3
  342.3 6.9 collective-permute-done
  349.2 44.2 %fusion.90 = (f32[2,4,2048]{2,1,0:T(4,128)S(1)}, f32[2,2048,2048,4]{2,1,3,0:T(8,128)}) fusion(pred[2048,2048]{0,1:T(8,128)(4,1)S(1)} %broadcast_compare_fusion.3, bf16[2048,2,4,32]{0,3,2,1:T(8,128)(2,1)S(1)} %get-tuple-element.402, bf16[2048,2,32]{0,2,1:T(8,128)(2,1)S(1)} %collective-permute-done), kind=kOutput, calls=%fused_computation.8.clone.1 | convolution fusion | flops 2248130560 | bytes 139788288 | tf_op jit(solution)/shard_map/while/body/eval_jaxpr/qgrd,kgd->grqk/dot_general | solution.py:15
  393.4 0.9 max.12
  394.3 42.4 %fusion.91 = f32[2,4,2048]{2,1,0:T(4,128)S(1)} fusion(f32[2,2048,2048,4]{2,1,3,0:T(8,128)} %get-tuple-element.360, f32[2,4,2048]{2,1,0:T(4,128)S(1)} %max.12, pred[2048,2048]{0,1:T(8,128)(4,1)} %copy-done.1), kind=kLoop, calls=%fused_computation.7.clone.1 | loop fusion | flops 134201344 | bytes 138543104 | tf_op jit(solution)/shard_map/while/body/eval_jaxpr/reduce_sum | solution.py:21
  436.7 0.9 multiply_add_fusion.4
  438.3 47.9 %multiply_add_fusion.5 = f32[2,4,2048,32]{2,3,1,0:T(8,128)} fusion(f32[2,4,2048,32]{2,3,1,0:T(8,128)} %get-tuple-element.384, f32[2,4,2048]{2,1,0:T(4,128)S(1)} %bitcast.226, f32[2,2048,2048,4]{2,1,3,0:T(8,128)} %get-tuple-element.360, f32[2,4,2048]{2,1,0:T(4,128)S(1)} %max.12, pred[2048,2048]{0,1:T(8,128)(4,1)} %copy-done.1, ...), kind=kOutput, calls=%fused_computation.12.clone.1 | convolution fusion | flops 2282749952 | bytes 142999552 | tf_op jit(solution)/shard_map/while/body/eval_jaxpr/grqk,kgd->grqd/dot_general | solution.py:22
  486.3 2.9 broadcast_compare_fusion.3
  489.2 5.8 collective-permute-done
  495.0 44.2 %fusion.90 = (f32[2,4,2048]{2,1,0:T(4,128)S(1)}, f32[2,2048,2048,4]{2,1,3,0:T(8,128)}) fusion(pred[2048,2048]{0,1:T(8,128)(4,1)S(1)} %broadcast_compare_fusion.3, bf16[2048,2,4,32]{0,3,2,1:T(8,128)(2,1)S(1)} %get-tuple-element.402, bf16[2048,2,32]{0,2,1:T(8,128)(2,1)S(1)} %collective-permute-done), kind=kOutput, calls=%fused_computation.8.clone.1 | convolution fusion | flops 2248130560 | bytes 139788288 | tf_op jit(solution)/shard_map/while/body/eval_jaxpr/qgrd,kgd->grqk/dot_general | solution.py:15
  539.2 0.9 max.12
  540.1 42.4 %fusion.91 = f32[2,4,2048]{2,1,0:T(4,128)S(1)} fusion(f32[2,2048,2048,4]{2,1,3,0:T(8,128)} %get-tuple-element.360, f32[2,4,2048]{2,1,0:T(4,128)S(1)} %max.12, pred[2048,2048]{0,1:T(8,128)(4,1)} %copy-done.1), kind=kLoop, calls=%fused_computation.7.clone.1 | loop fusion | flops 134201344 | bytes 138543104 | tf_op jit(solution)/shard_map/while/body/eval_jaxpr/reduce_sum | solution.py:21
  582.5 0.9 multiply_add_fusion.4
  584.1 47.9 %multiply_add_fusion.5 = f32[2,4,2048,32]{2,3,1,0:T(8,128)} fusion(f32[2,4,2048,32]{2,3,1,0:T(8,128)} %get-tuple-element.384, f32[2,4,2048]{2,1,0:T(4,128)S(1)} %bitcast.226, f32[2,2048,2048,4]{2,1,3,0:T(8,128)} %get-tuple-element.360, f32[2,4,2048]{2,1,0:T(4,128)S(1)} %max.12, pred[2048,2048]{0,1:T(8,128)(4,1)} %copy-done.1, ...), kind=kOutput, calls=%fused_computation.12.clone.1 | convolution fusion | flops 2282749952 | bytes 142999552 | tf_op jit(solution)/shard_map/while/body/eval_jaxpr/grqk,kgd->grqd/dot_general | solution.py:22
  632.0 6.1 convolution_bitcast_fusion
  638.2 0.7 copy-done.8
  639.3 2.3 reduce-window.6
  642.5 8.0 scatter_custom_fusion
  650.6 55.7 %reduce-scatter.2.cloned.1.call-done = f32[512,1024]{1,0:T(8,128)} async-done(((f32[2048,1024]{1,0:T(8,128)}), f32[512,1024]{1,0:T(8,128)}) %reduce-scatter.2.cloned.1.call-update) | async-done | bytes 2097168 | tf_op jit(solution)/shard_map/reduce_scatter | solution.py:70
  706.3 1.9 add_convert_fusion.1
  708.3 5.4 gather_fusion
  713.6 1.9 broadcast_select_fusion.1
  716.3 50.7 %all_to_all.20 = bf16[4,4,1,128,1024]{4,3,0,2,1:T(8,128)(2,1)S(1)} all-to-all(bf16[4,4,1,128,1024]{4,3,0,2,1:T(8,128)(2,1)S(1)} %bitcast.219), channel_id=1, replica_groups=mesh['dp'=2,'cp'=4,'tp'=4] {'tp'}, dimensions={1} | all-to-all | bytes 8388608 | tf_op jit(solution)/shard_map/all_to_all | solution.py:81
  767.0 2.4 copy.43
  769.3 4.9 all-to-all-start.1
  774.2 92.7 %all-to-all-done.1 = bf16[4,4,1,128,1024]{4,3,1,2,0:T(8,128)(2,1)} async-done(((bf16[4,4,1,128,1024]{4,3,1,2,0:T(8,128)(2,1)}), bf16[4,4,1,128,1024]{4,3,1,2,0:T(8,128)(2,1)}, u32[]{:S(2)}, u32[]{:S(2)}) %all-to-all-start.1) | async-done | bytes 4194336 | tf_op jit(solution)/shard_map/all_to_all | solution.py:82
  866.9 13.6 %fusion.30 = f32[4,4,128,1792]{3,2,1,0:T(8,128)} fusion(bf16[4,4,1,128,1024]{4,3,1,2,0:T(8,128)(2,1)} %all-to-all-done.1, bf16[1,1024,1792]{2,1,0:T(8,128)(2,1)} %param.20), kind=kOutput, calls=%fused_computation.43 | convolution fusion | flops 7516192768 | bytes 22544384 | tf_op jit(solution)/shard_map/uvech,ehf->uvecf/dot_general | solution.py:85
  880.5 23.9 %fusion.26 = f32[4,4,128,1024]{3,2,1,0:T(8,128)} fusion(f32[4,4,128,1792]{3,2,1,0:T(8,128)} %fusion.30, bf16[1,1792,1024]{2,1,0:T(8,128)(2,1)} %param.21, bf16[4,4,1,128,1024]{4,3,1,2,0:T(8,128)(2,1)} %all-to-all-done.1, bf16[1,1024,1792]{2,1,0:T(8,128)(2,1)} %param.19), kind=kOutput, calls=%fused_computation.38 | convolution fusion | flops 15054405632 | bytes 34603008 | tf_op jit(solution)/shard_map/uvecf,efh->uvech/dot_general | solution.py:87
  904.4 4.8 dynamic-slice_bitcast_fusion
  909.2 7.1 collective-permute-done.2
  916.3 4.2 fusion.42
  920.5 55.5 %all_to_all.21 = bf16[4,4,1,128,512]{4,3,1,2,0:T(8,128)(2,1)S(1)} all-to-all(bf16[4,4,1,128,512]{4,3,1,2,0:T(8,128)(2,1)S(1)} %fusion.42), channel_id=1, replica_groups=mesh['dp'=2,'cp'=4,'tp'=4] {'cp'}, dimensions={0} | all-to-all | bytes 4194304 | tf_op jit(solution)/shard_map/all_to_all | solution.py:95
  976.1 1.5 copy.45
  977.6 4.6 all-to-all-start.3
  982.9 24.7 %all-to-all-done.3 = bf16[4,4,1,128,512]{4,3,0,2,1:T(8,128)(2,1)} async-done(((bf16[4,4,1,128,512]{4,3,0,2,1:T(8,128)(2,1)}), bf16[4,4,1,128,512]{4,3,0,2,1:T(8,128)(2,1)}, u32[]{:S(2)}, u32[]{:S(2)}) %all-to-all-start.3) | async-done | bytes 2097184 | tf_op jit(solution)/shard_map/all_to_all | solution.py:96
  1007.6 3.7 copy.46
  1011.3 1.9 copy.58
  1013.2 7.9 gather_fusion.1
  1021.1 4.1 gather.15
  1025.2 10.1 multiply_reduce_fusion
  1035.3 1.4 add_convert_fusion
  (73 shorter events, 4.4 us)
Async XLA Ops:
  6.5 625.5 %copy-start = (bf16[8,32,1024]{2,1,0:T(8,128)(2,1)S(1)}, bf16[8,32,1024]{2,1,0:T(8,128)(2,1)}, u32[]{:S(2)}) copy-start(bf16[8,32,1024]{2,1,0:T(8,128)(2,1)} %param.16) | copy-start | bytes 1572868
  6.5 39.4 %copy-start.10 = (bf16[1024,8,32]{0,2,1:T(8,128)(2,1)S(1)}, bf16[1024,8,32]{0,2,1:T(8,128)(2,1)}, u32[]{:S(2)}) copy-start(bf16[1024,8,32]{0,2,1:T(8,128)(2,1)} %param.13) | copy-start | bytes 1572868
  6.5 39.4 %all-gather.2.cloned.1.call-start = ((), (), s32[]{:S(2)}) async-start(), calls=%async_computation.5 | async-start | bytes 5242880 | tf_op jit(solution)/shard_map/all_gather | solution.py:46
  7.3 699.1 %reduce-scatter.2.cloned.1.call-start = ((), (), s32[]{:S(2)}) async-start(), calls=%async_computation.6 | async-start | bytes 10485760 | tf_op jit(solution)/shard_map/reduce_scatter | solution.py:70
  11.5 38.1 %copy-start.6 = (bf16[1024,2,32]{0,2,1:T(8,128)(2,1)S(1)}, bf16[1024,2,32]{0,2,1:T(8,128)(2,1)}, u32[]{:S(2)}) copy-start(bf16[1024,2,32]{0,2,1:T(8,128)(2,1)} %param.14) | copy-start | bytes 393220
  46.0 3.7 copy-start.2
  49.6 2.2 copy-start.3
  96.6 42.7 %copy-start.7 = (bf16[1024,2,32]{0,2,1:T(8,128)(2,1)S(1)}, bf16[1024,2,32]{0,2,1:T(8,128)(2,1)}, u32[]{:S(2)}) copy-start(bf16[1024,2,32]{0,2,1:T(8,128)(2,1)} %param.15) | copy-start | bytes 393220
  139.2 3.8 copy-start.4
  190.2 11.0 %collective-permute-start = (bf16[2048,2,32]{0,2,1:T(8,128)(2,1)S(1)}, bf16[2048,2,32]{0,2,1:T(8,128)(2,1)S(1)}, u32[]{:S(2)}, u32[]{:S(2)}) collective-permute-start(bf16[2048,2,32]{0,2,1:T(8,128)(2,1)S(1)} %get-tuple-element.380), channel_id=1, source_target_pairs={{0,4},{4,8},{8,12},{12,0},{1,5},{5,9},{9,13},{13,1},{2,6},{6,10},{... | collective-permute-start | bytes 786440 | tf_op jit(solution)/shard_map/while/body/eval_jaxpr/ppermute | solution.py:60
  191.7 98.6 %collective-permute-start.1 = (bf16[2048,2,32]{0,2,1:T(8,128)(2,1)S(1)}, bf16[2048,2,32]{0,2,1:T(8,128)(2,1)S(1)}, u32[]{:S(2)}, u32[]{:S(2)}) collective-permute-start(bf16[2048,2,32]{0,2,1:T(8,128)(2,1)S(1)} %get-tuple-element.381), channel_id=1, source_target_pairs={{0,4},{4,8},{8,12},{12,0},{1,5},{5,9},{9,13},{13,1},{2,6},{6,10},{... | collective-permute-start | bytes 786440 | tf_op jit(solution)/shard_map/while/body/eval_jaxpr/ppermute | solution.py:61
  196.1 49.3 %copy-start.1 = (pred[2048,2048]{0,1:T(8,128)(4,1)}, pred[2048,2048]{0,1:T(8,128)(4,1)S(1)}, u32[]{:S(2)}) copy-start(pred[2048,2048]{0,1:T(8,128)(4,1)S(1)} %broadcast_compare_fusion.3) | copy-start | bytes 12582916 | tf_op jit(solution)/shard_map/while
  338.2 11.0 %collective-permute-start = (bf16[2048,2,32]{0,2,1:T(8,128)(2,1)S(1)}, bf16[2048,2,32]{0,2,1:T(8,128)(2,1)S(1)}, u32[]{:S(2)}, u32[]{:S(2)}) collective-permute-start(bf16[2048,2,32]{0,2,1:T(8,128)(2,1)S(1)} %get-tuple-element.380), channel_id=1, source_target_pairs={{0,4},{4,8},{8,12},{12,0},{1,5},{5,9},{9,13},{13,1},{2,6},{6,10},{... | collective-permute-start | bytes 786440 | tf_op jit(solution)/shard_map/while/body/eval_jaxpr/ppermute | solution.py:60
  338.2 100.0 %collective-permute-start.1 = (bf16[2048,2,32]{0,2,1:T(8,128)(2,1)S(1)}, bf16[2048,2,32]{0,2,1:T(8,128)(2,1)S(1)}, u32[]{:S(2)}, u32[]{:S(2)}) collective-permute-start(bf16[2048,2,32]{0,2,1:T(8,128)(2,1)S(1)} %get-tuple-element.381), channel_id=1, source_target_pairs={{0,4},{4,8},{8,12},{12,0},{1,5},{5,9},{9,13},{13,1},{2,6},{6,10},{... | collective-permute-start | bytes 786440 | tf_op jit(solution)/shard_map/while/body/eval_jaxpr/ppermute | solution.py:61
  342.3 51.1 %copy-start.1 = (pred[2048,2048]{0,1:T(8,128)(4,1)}, pred[2048,2048]{0,1:T(8,128)(4,1)S(1)}, u32[]{:S(2)}) copy-start(pred[2048,2048]{0,1:T(8,128)(4,1)S(1)} %broadcast_compare_fusion.3) | copy-start | bytes 12582916 | tf_op jit(solution)/shard_map/while
  486.2 8.8 collective-permute-start
  486.2 97.8 %collective-permute-start.1 = (bf16[2048,2,32]{0,2,1:T(8,128)(2,1)S(1)}, bf16[2048,2,32]{0,2,1:T(8,128)(2,1)S(1)}, u32[]{:S(2)}, u32[]{:S(2)}) collective-permute-start(bf16[2048,2,32]{0,2,1:T(8,128)(2,1)S(1)} %get-tuple-element.381), channel_id=1, source_target_pairs={{0,4},{4,8},{8,12},{12,0},{1,5},{5,9},{9,13},{13,1},{2,6},{6,10},{... | collective-permute-start | bytes 786440 | tf_op jit(solution)/shard_map/while/body/eval_jaxpr/ppermute | solution.py:61
  489.2 50.0 %copy-start.1 = (pred[2048,2048]{0,1:T(8,128)(4,1)}, pred[2048,2048]{0,1:T(8,128)(4,1)S(1)}, u32[]{:S(2)}) copy-start(pred[2048,2048]{0,1:T(8,128)(4,1)S(1)} %broadcast_compare_fusion.3) | copy-start | bytes 12582916 | tf_op jit(solution)/shard_map/while
  638.1 0.7 copy-start.8
  638.1 68.2 %copy-start.5 = (bf16[512,1024]{1,0:T(8,128)(2,1)S(1)}, bf16[512,1024]{1,0:T(8,128)(2,1)}, u32[]{:S(2)}) copy-start(bf16[512,1024]{1,0:T(8,128)(2,1)} %param.12) | copy-start | bytes 3145732
  769.3 97.6 %all-to-all-start.1 = ((bf16[4,4,1,128,1024]{4,3,1,2,0:T(8,128)(2,1)}), bf16[4,4,1,128,1024]{4,3,1,2,0:T(8,128)(2,1)}, u32[]{:S(2)}, u32[]{:S(2)}) async-start(bf16[4,4,1,128,1024]{4,3,1,2,0:T(8,128)(2,1)} %copy.43), calls=%async_computation.2 | async-start | bytes 8388608 | tf_op jit(solution)/shard_map/all_to_all | solution.py:82
  909.2 7.1 collective-permute-start.2
  976.1 6.7 copy-start.9
  977.6 30.0 %all-to-all-start.3 = ((bf16[4,4,1,128,512]{4,3,0,2,1:T(8,128)(2,1)}), bf16[4,4,1,128,512]{4,3,0,2,1:T(8,128)(2,1)}, u32[]{:S(2)}, u32[]{:S(2)}) async-start(bf16[4,4,1,128,512]{4,3,0,2,1:T(8,128)(2,1)} %copy.45), calls=%async_computation.4 | async-start | bytes 4194304 | tf_op jit(solution)/shard_map/all_to_all | solution.py:96
Sparse Core Ops, SparseCore 0:
  8.9 37.0 all-gather.1
  638.3 67.9 reduce-scatter.1
where the time goes:
time: 1050 us; the launch traced here: 1040 us
  matrix products  420 us (40%)
  waiting for transfers between devices  233 us (22%)
  other arithmetic  219 us (21%)
  blocking collectives  106 us (10%)
  local copies, waits for them, and re-layouts  37.6 us (4%)
  between operations  13.9 us (1%)
  starting transfers between devices  13.7 us (1%)
    dot_general x4, matrix products, attend_block(): jnp.einsum('grqk,kgd->grqd', prob_vals.astype(jnp.bfloat16), v_blk, prefe...  191 us
    dot_general x4, matrix products, attend_block(): jnp.einsum('qgrd,kgd->grqk', q_loc, k_blk, preferred_element_type=jnp.flo...  177 us
    reduce_sum x4, other arithmetic, attend_block(): new_sum = run_sum * rescale + jnp.sum(prob_vals, axis=-1)  170 us
    all_to_all x1, waiting for transfers between devices, device_step(): recv_buf = lax.all_to_all(recv_buf, 'cp', 0, 0, tiled=True)  92.7 us
    reduce_scatter x1, waiting for transfers between devices, device_step(): lax.psum_scatter(attn_part, 'tp', scatter_dimension=0, tiled=True)  55.7 us
    all_to_all x1, blocking collectives, device_step(): back_buf = lax.all_to_all(z_half, 'cp', 0, 0, tiled=True)  55.5 us
    all_to_all x1, blocking collectives, device_step(): recv_buf = lax.all_to_all(send_buf, 'tp', 1, 1, tiled=True)  50.7 us
    all_gather x1, waiting for transfers between devices, device_step(): x_half = lax.all_gather(x_loc, 'tp', axis=0, tiled=True)  34.5 us
  transfers between devices with their start and end apart: 11, of which 8 were waited for; matrix products, arithmetic and copies ran while one was open for 28% of the time, Pallas kernels for 0%

commit v1 on v0

v1 whole, which is shorter than its diff:
```python
import functools
import math

import jax
import jax.numpy as jnp
from jax import lax
from jax.experimental import pallas as pl
from jax.experimental.pallas import tpu as pltpu
from jax.sharding import PartitionSpec as P


def attn_kernel(n_cp, chunk, bq, bk, heads, grp, q_ref, k_ref, v_ref, o_ref, m_ref, l_ref, acc_ref):
    head_dim = acc_ref.shape[1]
    cp_index = lax.axis_index("cp")
    step = pl.program_id(0)
    q_per = chunk // bq
    k_per = chunk // bk
    half = step // q_per
    in_chunk = step % q_per
    my_chunk = jnp.where(half == 0, cp_index, 2 * n_cp - 1 - cp_index)
    diag = (in_chunk * bq) // bk
    score_scale = head_dim ** -0.5 * math.log2(math.e)

    def key_offset(blk):
        chunk_id = blk // k_per
        rank = jnp.where(chunk_id < n_cp, chunk_id, 2 * n_cp - 1 - chunk_id)
        upper = jnp.where(chunk_id < n_cp, 0, 1)
        return rank * (2 * chunk) + upper * chunk + (blk % k_per) * bk

    def visit(blk, first):
        off = pl.multiple_of(key_offset(blk), bk)
        k_blk = k_ref[pl.ds(off, bk), :]
        v_blk = v_ref[:, pl.ds(off, bk)]
        if first:
            k_pos = diag * bk + lax.broadcasted_iota(jnp.int32, (bk, bq), 0)
            q_pos = in_chunk * bq + lax.broadcasted_iota(jnp.int32, (bk, bq), 1)
            allowed = k_pos <= q_pos
        for head in range(heads):
            kv = head // grp
            scores = jnp.dot(k_blk, q_ref[head], preferred_element_type=jnp.float32)
            if first:
                scores = jnp.where(allowed, scores, -1e30)
            top = jnp.max(scores, axis=0, keepdims=True)
            if not first:
                old = m_ref[head]
                top = jnp.maximum(old, top)
            prob = jnp.exp2((scores - top) * score_scale)
            part = jnp.sum(prob.reshape(bk // 8, 8, bq), axis=0)
            mixed = jnp.dot(v_blk[kv * head_dim:(kv + 1) * head_dim], prob.astype(jnp.bfloat16), preferred_element_type=jnp.float32)
            m_ref[head] = top
            if first:
                l_ref[head] = part
                acc_ref[head] = mixed
            else:
                rescale = jnp.exp2((old - top) * score_scale)
                l_ref[head] = l_ref[head] * rescale + part
                acc_ref[head] = acc_ref[head] * rescale + mixed

    base = my_chunk * k_per
    visit(base + diag, True)

    def body(blk, carry):
        visit(blk, False)
        return carry

    lax.fori_loop(0, base + diag, body, 0)
    for head in range(heads):
        total = jnp.sum(l_ref[head], axis=0, keepdims=True)
        o_ref[head] = (acc_ref[head] / total).astype(o_ref.dtype)


def attention(q_t, k_all, v_all, n_cp, head_dim, bq=256, bk=512):
    heads, depth, rows = q_t.shape
    chunk = rows // 2
    n_keys = k_all.shape[0]
    grp = heads // (depth // head_dim)
    pairs = heads * rows * n_keys // 2
    return pl.pallas_call(
        functools.partial(attn_kernel, n_cp, chunk, bq, bk, heads, grp),
        out_shape=jax.ShapeDtypeStruct((heads, head_dim, rows), jnp.bfloat16),
        grid=(rows // bq,),
        in_specs=[
            pl.BlockSpec((heads, depth, bq), lambda i: (0, 0, i)),
            pl.BlockSpec((n_keys, depth), lambda i: (0, 0)),
            pl.BlockSpec((depth, n_keys), lambda i: (0, 0)),
        ],
        out_specs=pl.BlockSpec((heads, head_dim, bq), lambda i: (0, 0, i)),
        scratch_shapes=[
            pltpu.VMEM((heads, 1, bq), jnp.float32),
            pltpu.VMEM((heads, 8, bq), jnp.float32),
            pltpu.VMEM((heads, head_dim, bq), jnp.float32),
        ],
        compiler_params=pltpu.CompilerParams(dimension_semantics=("arbitrary",), vmem_limit_bytes=48 * 1024 * 1024),
        cost_estimate=pl.CostEstimate(flops=4 * pairs * 64, bytes_accessed=8 * 1024 * 1024, transcendentals=pairs),
        name="causal_attention",
    )(q_t, k_all, v_all)


def solution(mesh):
    n_cp = mesh.shape["cp"]
    n_tp = mesh.shape["tp"]
    row_spec = P(("dp", "cp", "tp"), None)
    head_spec = P(None, "tp", None)
    expert_spec = P(("cp", "tp"), None, None)

    def device_step(x_loc, w_q, w_k, w_v, w_o, ids_loc, gates_loc, w_gate, w_up, w_down):
        tok_dev, hid_dim = x_loc.shape
        top_k = ids_loc.shape[1]
        kv_loc = w_k.shape[1]
        heads = w_q.shape[1]
        head_dim = w_q.shape[2]
        grp_size = heads // kv_loc
        local_exp = w_gate.shape[0]
        n_experts = local_exp * n_cp * n_tp // 2
        capacity = top_k * tok_dev // n_experts
        half_hid = hid_dim // 2
        tp_index = lax.axis_index("tp")
        n_slots = n_experts * capacity

        choice_hot = (ids_loc[:, :, None] == jnp.arange(n_experts)[None, None, :])
        token_hot = jnp.sum(choice_hot.astype(jnp.bfloat16), axis=1)
        earlier = (lax.broadcasted_iota(jnp.int32, (tok_dev, tok_dev), 0) > lax.broadcasted_iota(jnp.int32, (tok_dev, tok_dev), 1)).astype(jnp.bfloat16)
        rank_in = jnp.dot(earlier, token_hot, preferred_element_type=jnp.float32).astype(jnp.int32)
        place = rank_in + jnp.arange(n_experts, dtype=jnp.int32)[None, :] * capacity
        dest_idx = jnp.sum(jnp.where(choice_hot, place[:, None, :], 0), axis=2)

        x_half = lax.all_gather(x_loc, "tp", axis=0, tiled=True)
        half_len = x_half.shape[0]
        q_t = jnp.einsum("sh,hnd->nds", x_half, w_q, preferred_element_type=jnp.float32).astype(jnp.bfloat16)
        q_t = q_t.reshape(kv_loc, grp_size, head_dim, half_len)
        q_t = jnp.concatenate([jnp.pad(q_t[kv], ((0, 0), (kv * head_dim, (kv_loc - 1 - kv) * head_dim), (0, 0))) for kv in range(kv_loc)], axis=0)
        k_cur = jnp.einsum("sh,hnd->snd", x_half, w_k, preferred_element_type=jnp.float32).astype(jnp.bfloat16).reshape(half_len, kv_loc * head_dim)
        v_cur = jnp.einsum("sh,hnd->nds", x_half, w_v, preferred_element_type=jnp.float32).astype(jnp.bfloat16).reshape(kv_loc * head_dim, half_len)
        k_all = lax.all_gather(k_cur, "cp", axis=0, tiled=True)
        v_all = lax.all_gather(v_cur, "cp", axis=1, tiled=True)
        out_t = attention(q_t, k_all, v_all, n_cp, head_dim)
        out_t = out_t.reshape(heads * head_dim, n_tp, tok_dev)
        out_t = lax.all_to_all(out_t, "tp", 1, 0, tiled=True).reshape(n_tp * heads * head_dim, tok_dev)
        w_o_all = lax.all_gather(w_o.reshape(heads * head_dim, hid_dim), "tp", axis=0, tiled=True)
        attn_rows = lax.dot_general(out_t, w_o_all, (((0,), (0,)), ((), ())), preferred_element_type=jnp.float32)
        h_loc = (x_loc.astype(jnp.float32) + attn_rows).astype(jnp.bfloat16)

        slots = jnp.arange(n_slots, dtype=jnp.int32)
        pick = (slots[:, None] == dest_idx[:, 0][None, :]) | (slots[:, None] == dest_idx[:, 1][None, :])
        send_buf = jnp.dot(pick.astype(jnp.bfloat16), h_loc, preferred_element_type=jnp.float32).astype(jnp.bfloat16)
        send_buf = send_buf.reshape(n_cp, n_tp // 2, 1, local_exp, capacity, hid_dim)
        send_buf = jnp.broadcast_to(send_buf, (n_cp, n_tp // 2, 2, local_exp, capacity, hid_dim)).reshape(n_cp, n_tp, local_exp, capacity, hid_dim)
        recv_buf = lax.all_to_all(send_buf, "tp", 1, 1, tiled=True)
        recv_buf = lax.all_to_all(recv_buf, "cp", 0, 0, tiled=True)

        gate_pre = jnp.einsum("uvech,ehf->uvecf", recv_buf, w_gate, preferred_element_type=jnp.float32)
        up_pre = jnp.einsum("uvech,ehf->uvecf", recv_buf, w_up, preferred_element_type=jnp.float32)
        hidden = (jax.nn.silu(gate_pre) * up_pre).astype(jnp.bfloat16)
        z_part = jnp.einsum("uvecf,efh->uvech", hidden, w_down, preferred_element_type=jnp.float32)

        my_half = tp_index % 2
        keep_part = lax.dynamic_slice_in_dim(z_part, my_half * half_hid, half_hid, axis=4)
        send_part = lax.dynamic_slice_in_dim(z_part, (1 - my_half) * half_hid, half_hid, axis=4)
        pair_perm = [(dev_idx, dev_idx ^ 1) for dev_idx in range(n_tp)]
        z_half = (keep_part + lax.ppermute(send_part, "tp", pair_perm)).astype(jnp.bfloat16)

        back_buf = lax.all_to_all(z_half, "cp", 0, 0, tiled=True)
        back_buf = lax.all_to_all(back_buf, "tp", 1, 1, tiled=True)
        z_full = back_buf.reshape(n_cp, n_tp // 2, 2, local_exp, capacity, half_hid).transpose(0, 1, 3, 4, 2, 5).reshape(n_slots, hid_dim)
        y_loc = h_loc.astype(jnp.float32)
        for choice in range(top_k):
            take = (dest_idx[:, choice][:, None] == slots[None, :]).astype(jnp.bfloat16)
            y_loc = y_loc + gates_loc[:, choice:choice + 1] * jnp.dot(take, z_full, preferred_element_type=jnp.float32)
        return y_loc.astype(jnp.bfloat16)

    return jax.shard_map(device_step, mesh=mesh, in_specs=(row_spec, head_spec, head_spec, head_spec, P("tp", None, None), row_spec, row_spec, expert_spec, expert_spec, expert_spec), out_specs=row_spec, check_vma=False)
```

time: 1050 us -> 680 us (0.65)
  matrix products: 420 us -> 57 us
  Pallas kernels: 0 us -> 226 us
  other arithmetic: 219 us -> 4.53 us
  local copies, waits for them, and re-layouts: 37.6 us -> 16.6 us
  waiting for transfers between devices: 233 us -> 244 us
    dot_general x9 -> x7, matrix products: 374 us -> 15.9 us  [the longest x1 4.29 us: device_step(): jnp.einsum('sh,hnd->nds', x_half, w_v, preferred_element_type=jnp.float32)]
    pallas_call x0 -> x1, Pallas kernels: none -> 226 us  [attention(): pl.pallas_call(functools.partial(attn_kernel, n_cp, chunk, bq, bk, heads,...]
    reduce_sum x6 -> x2, other arithmetic: 180 us -> 0.06 us  [the longest x1 0.05 us: device_step(): dest_idx = jnp.sum(jnp.where(choice_hot, place[:, None, :], 0), axis=2)]
    all_gather x0 -> x3, waiting for transfers between devices: none -> 65.2 us  [the longest x1 36.6 us: device_step(): k_all = lax.all_gather(k_cur, 'cp', axis=0, tiled=True)]
    reduce_scatter x1 -> x0, waiting for transfers between devices: 55.7 us -> none  [device_step(): lax.psum_scatter(attn_part, 'tp', scatter_dimension=0, tiled=True)]
    ppermute x6 -> x0, waiting for transfers between devices: 17.8 us -> none  [the longest x3 17.8 us: kv_step(): k_blk = lax.ppermute(k_blk, 'cp', shift_perm)]
    gather x3 -> x0, local copies, waits for them, and re-layouts: 17.4 us -> none  [the longest x2 12 us: device_step(): picked = jnp.take(z_full, dest_idx, axis=0).reshape(tok_dev, top_k, hid_dim)]
    all_to_all x0 -> x1, waiting for transfers between devices: none -> 13.7 us  [device_step(): lax.all_to_all(out_t, 'tp', 1, 0, tiled=True)]
  transfers between devices with their start and end apart: 11 -> 8, of which waited for: 8 -> 7; matrix products, arithmetic and copies ran while one was open for 28% -> 2% of each run, Pallas kernels for 0% -> 33%
where the time goes in v1:
time: 680 us
  waiting for transfers between devices  244 us (36%)
  Pallas kernels  226 us (33%)
  blocking collectives  106 us (16%)
  matrix products  57 us (8%)
  local copies, waits for them, and re-layouts  16.6 us (2%)
  between operations  13.4 us (2%)
  starting transfers between devices  12.5 us (2%)
    pallas_call x1, Pallas kernels, attention(): pl.pallas_call(functools.partial(attn_kernel, n_cp, chunk, bq, bk, heads,...  226 us
    all_to_all x1, waiting for transfers between devices, device_step(): recv_buf = lax.all_to_all(recv_buf, 'cp', 0, 0, tiled=True)  92.7 us
    all_to_all x1, blocking collectives, device_step(): back_buf = lax.all_to_all(z_half, 'cp', 0, 0, tiled=True)  55.5 us
    all_to_all x1, blocking collectives, device_step(): recv_buf = lax.all_to_all(send_buf, 'tp', 1, 1, tiled=True)  50.7 us
    all_gather x1, waiting for transfers between devices, device_step(): x_half = lax.all_gather(x_loc, 'tp', axis=0, tiled=True)  38.7 us
    all_gather x1, waiting for transfers between devices, device_step(): k_all = lax.all_gather(k_cur, 'cp', axis=0, tiled=True)  36.6 us
    all_gather x1, waiting for transfers between devices, device_step(): v_all = lax.all_gather(v_cur, 'cp', axis=1, tiled=True)  28.5 us
    all_to_all x1, waiting for transfers between devices, device_step(): back_buf = lax.all_to_all(back_buf, 'tp', 1, 1, tiled=True)  25.2 us
  transfers between devices with their start and end apart: 8, of which 7 were waited for; matrix products, arithmetic and copies ran while one was open for 2% of the time, Pallas kernels for 33%

profile of v1, /device:TPU:0, one launch (start us, length us, event | category | flops | bytes accessed | tf_op | source)
XLA Modules:
  0.0 679.6 jit_solution(3954015867495159052)
XLA Ops:
  6.5 0.0 copy-start
  6.5 0.0 all-gather.5.cloned.1.call-start
  6.5 0.7 all-gather.5.cloned.1.call-update
  7.3 0.0 all-gather.7.cloned.1.call-start
  7.3 38.7 %all-gather.5.cloned.1.call-done = bf16[2048,1024]{1,0:T(8,128)(2,1)} async-done(((bf16[512,1024]{1,0:T(8,128)(2,1)}), bf16[2048,1024]{1,0:T(8,128)(2,1)}) %all-gather.5.cloned.1.call-update) | async-done | bytes 4194320 | tf_op jit(solution)/shard_map/all_gather | solution.py:127
  46.0 0.0 copy-start.4
  46.0 3.6 fusion.53
  49.6 1.0 copy.28
  50.6 0.0 all-gather.7.cloned.1.call-update
  50.7 0.0 all-gather.9.cloned.1.call-start
  50.7 0.0 copy-done.4
  50.7 4.3 fusion.29
  55.0 0.0 all-gather.9.cloned.1.call-update
  55.0 0.0 all-gather.11.cloned.1.call-start
  55.1 0.5 all-gather.11.cloned.1.call-update
  55.6 0.0 copy-done
  55.6 3.5 fusion.26
  59.1 0.1 fusion.50
  59.2 0.2 fusion.32.q_ref
  59.4 36.6 %all-gather.7.cloned.1.call-done.k_ref = bf16[8192,64]{1,0:T(8,128)(2,1)} async-done(((bf16[2048,64]{1,0:T(8,128)(2,1)}), bf16[8192,64]{1,0:T(8,128)(2,1)}) %all-gather.7.cloned.1.call-update) | async-done | bytes 1048592 | tf_op jit(solution)/shard_map/all_gather | solution.py:134
  96.1 28.5 %all-gather.9.cloned.1.call-done.v_ref = bf16[64,8192]{1,0:T(8,128)(2,1)} async-done(((bf16[64,2048]{1,0:T(8,128)(2,1)}), bf16[64,8192]{1,0:T(8,128)(2,1)}) %all-gather.9.cloned.1.call-update) | async-done | bytes 1048592 | tf_op jit(solution)/shard_map/all_gather | solution.py:135
  124.6 0.0 copy-start.2
  124.6 1.2 copy-done.2
  125.8 225.6 %causal_attention.1 = bf16[8,32,2048]{2,1,0:T(8,128)(2,1)S(1)} custom-call(bf16[8,64,2048]{2,1,0:T(8,128)(2,1)S(1)} %fusion.32.q_ref, bf16[8192,64]{1,0:T(8,128)(2,1)} %all-gather.7.cloned.1.call-done.k_ref, bf16[64,8192]{1,0:T(8,128)(2,1)S(1)} %copy-done.2), custom_call_target="tpu_custom_call" | custom-call | flops 17179869184 | bytes 8388608 | tf_op jit(solution)/shard_map/causal_attention/pallas_call | solution.py:78
  351.4 0.0 copy-start.5
  351.5 0.0 copy-start.3
  351.5 0.8 reshape.71
  352.3 1.2 copy.29
  353.4 3.7 all-to-all-start
  357.1 0.0 copy-done.5
  357.2 0.2 fusion.42
  357.4 0.1 select_reduce_fusion
  357.5 0.0 all-gather.11.cloned.1.call-done
  357.5 13.7 %all-to-all-done = bf16[256,4,512]{2,0,1:T(8,128)(2,1)S(1)} async-done(((bf16[256,4,512]{2,0,1:T(8,128)(2,1)}), bf16[256,4,512]{2,0,1:T(8,128)(2,1)S(1)}, u32[]{:S(2)}, u32[]{:S(2)}) %all-to-all-start) | async-done | bytes 1048608 | tf_op jit(solution)/shard_map/all_to_all | solution.py:138
  371.1 0.0 copy-done.3
  371.1 2.9 add_convert_fusion.1
  374.0 1.3 fusion.39
  375.3 0.3 copy.30
  375.6 0.6 broadcast_in_dim.32
  376.2 50.7 %all_to_all.35 = bf16[4,4,1,128,1024]{4,3,0,2,1:T(8,128)(2,1)S(1)} all-to-all(bf16[4,4,1,128,1024]{4,3,0,2,1:T(8,128)(2,1)S(1)} %bitcast.124), channel_id=1, replica_groups=mesh['dp'=2,'cp'=4,'tp'=4] {'tp'}, dimensions={1} | all-to-all | bytes 8388608 | tf_op jit(solution)/shard_map/all_to_all | solution.py:148
  426.9 2.4 copy.31
  429.2 4.8 all-to-all-start.2
  434.1 92.7 %all-to-all-done.2 = bf16[4,4,1,128,1024]{4,3,1,2,0:T(8,128)(2,1)} async-done(((bf16[4,4,1,128,1024]{4,3,1,2,0:T(8,128)(2,1)}), bf16[4,4,1,128,1024]{4,3,1,2,0:T(8,128)(2,1)}, u32[]{:S(2)}, u32[]{:S(2)}) %all-to-all-start.2) | async-done | bytes 4194336 | tf_op jit(solution)/shard_map/all_to_all | solution.py:149
  526.8 13.6 %fusion.8 = f32[4,4,128,1792]{3,2,1,0:T(8,128)} fusion(bf16[4,4,1,128,1024]{4,3,1,2,0:T(8,128)(2,1)} %all-to-all-done.2, bf16[1,1024,1792]{2,1,0:T(8,128)(2,1)} %param.18), kind=kOutput, calls=%fused_computation.13 | convolution fusion | flops 7516192768 | bytes 22544384 | tf_op jit(solution)/shard_map/uvech,ehf->uvecf/dot_general | solution.py:152
  540.3 23.9 %fusion.4 = f32[4,4,128,1024]{3,2,1,0:T(8,128)} fusion(f32[4,4,128,1792]{3,2,1,0:T(8,128)} %fusion.8, bf16[1,1792,1024]{2,1,0:T(8,128)(2,1)} %param.19, bf16[4,4,1,128,1024]{4,3,1,2,0:T(8,128)(2,1)} %all-to-all-done.2, bf16[1,1024,1792]{2,1,0:T(8,128)(2,1)} %param.17), kind=kOutput, calls=%fused_computation.7 | convolution fusion | flops 15054405632 | bytes 34603008 | tf_op jit(solution)/shard_map/uvecf,efh->uvech/dot_general | solution.py:154
  564.3 4.8 dynamic-slice_bitcast_fusion
  569.1 0.0 collective-permute-start
  569.1 7.1 %collective-permute-done = f32[4,4,1,128,512]{4,3,1,0,2:T(8,128)} collective-permute-done((f32[4,4,1,128,512]{4,3,1,0,2:T(8,128)}, f32[4,4,1,128,512]{4,3,1,0,2:T(8,128)}, u32[]{:S(2)}, u32[]{:S(2)}) %collective-permute-start) | collective-permute-done | bytes 4194336 | tf_op jit(solution)/shard_map/ppermute | solution.py:160
  576.2 4.2 fusion.33
  580.4 55.5 %all_to_all.36 = bf16[4,4,1,128,512]{4,3,1,2,0:T(8,128)(2,1)S(1)} all-to-all(bf16[4,4,1,128,512]{4,3,1,2,0:T(8,128)(2,1)S(1)} %fusion.33), channel_id=1, replica_groups=mesh['dp'=2,'cp'=4,'tp'=4] {'cp'}, dimensions={0} | all-to-all | bytes 4194304 | tf_op jit(solution)/shard_map/all_to_all | solution.py:162
  635.9 0.0 copy-start.6
  635.9 1.5 copy.33
  637.5 3.8 all-to-all-start.4
  641.3 0.0 copy-done.6
  641.3 25.2 %all-to-all-done.4 = bf16[4,4,1,128,512]{4,3,0,2,1:T(8,128)(2,1)S(1)} async-done(((bf16[4,4,1,128,512]{4,3,0,2,1:T(8,128)(2,1)}), bf16[4,4,1,128,512]{4,3,0,2,1:T(8,128)(2,1)S(1)}, u32[]{:S(2)}, u32[]{:S(2)}) %all-to-all-start.4) | async-done | bytes 2097184 | tf_op jit(solution)/shard_map/all_to_all | solution.py:163
  666.5 2.2 copy.34
  668.7 0.6 copy.38
  669.2 1.3 fusion.34
  670.6 0.0 copy-start.1
  670.6 2.5 add_convert_fusion
  673.0 0.0 copy-done.1
  (5 shorter events, 0.1 us)
Async XLA Ops:
  6.5 49.1 %copy-start = (bf16[1024,8,32]{0,2,1:T(8,128)(2,1)S(1)}, bf16[1024,8,32]{0,2,1:T(8,128)(2,1)}, u32[]{:S(2)}) copy-start(bf16[1024,8,32]{0,2,1:T(8,128)(2,1)} %param.11) | copy-start | bytes 1572868
  6.5 39.4 %all-gather.5.cloned.1.call-start = ((), (), s32[]{:S(2)}) async-start(), calls=%async_computation.5 | async-start | bytes 5242880 | tf_op jit(solution)/shard_map/all_gather | solution.py:127
  7.3 88.8 %all-gather.7.cloned.1.call-start = ((), (), s32[]{:S(2)}) async-start(), calls=%async_computation.6 | async-start | bytes 2621440 | tf_op jit(solution)/shard_map/all_gather | solution.py:134
  46.0 4.7 copy-start.4
  50.7 74.0 %all-gather.9.cloned.1.call-start = ((), (), s32[]{:S(2)}) async-start(), calls=%async_computation.7 | async-start | bytes 1310720 | tf_op jit(solution)/shard_map/all_gather | solution.py:135
  55.0 302.5 %all-gather.11.cloned.1.call-start = ((), (), s32[]{:S(2)}) async-start(), calls=%async_computation.8 | async-start | bytes 2621440 | tf_op jit(solution)/shard_map/all_gather | solution.py:139
  124.6 1.2 copy-start.2
  351.4 5.7 copy-start.5
  351.5 19.7 %copy-start.3 = (bf16[512,1024]{1,0:T(8,128)(2,1)S(1)}, bf16[512,1024]{1,0:T(8,128)(2,1)}, u32[]{:S(2)}) copy-start(bf16[512,1024]{1,0:T(8,128)(2,1)} %param.10) | copy-start | bytes 3145732
  353.4 17.7 %all-to-all-start = ((bf16[256,4,512]{2,0,1:T(8,128)(2,1)}), bf16[256,4,512]{2,0,1:T(8,128)(2,1)S(1)}, u32[]{:S(2)}, u32[]{:S(2)}) async-start(bf16[256,4,512]{2,0,1:T(8,128)(2,1)} %copy.29), calls=%async_computation | async-start | bytes 2097152 | tf_op jit(solution)/shard_map/all_to_all | solution.py:138
  429.2 97.6 %all-to-all-start.2 = ((bf16[4,4,1,128,1024]{4,3,1,2,0:T(8,128)(2,1)}), bf16[4,4,1,128,1024]{4,3,1,2,0:T(8,128)(2,1)}, u32[]{:S(2)}, u32[]{:S(2)}) async-start(bf16[4,4,1,128,1024]{4,3,1,2,0:T(8,128)(2,1)} %copy.31), calls=%async_computation.2 | async-start | bytes 8388608 | tf_op jit(solution)/shard_map/all_to_all | solution.py:149
  569.1 7.1 %collective-permute-start = (f32[4,4,1,128,512]{4,3,1,0,2:T(8,128)}, f32[4,4,1,128,512]{4,3,1,0,2:T(8,128)}, u32[]{:S(2)}, u32[]{:S(2)}) collective-permute-start(f32[4,4,1,128,512]{4,3,1,0,2:T(8,128)} %dynamic-slice_bitcast_fusion), channel_id=1, source_target_pairs={{0,1},{1,0},{2,3},{3,2},{4,5},{5,4},{6,7},{7,6},{8,9},{9,8},{10,11... | collective-permute-start | bytes 12582920 | tf_op jit(solution)/shard_map/ppermute | solution.py:160
  635.9 5.4 copy-start.6
  637.5 29.0 %all-to-all-start.4 = ((bf16[4,4,1,128,512]{4,3,0,2,1:T(8,128)(2,1)}), bf16[4,4,1,128,512]{4,3,0,2,1:T(8,128)(2,1)S(1)}, u32[]{:S(2)}, u32[]{:S(2)}) async-start(bf16[4,4,1,128,512]{4,3,0,2,1:T(8,128)(2,1)} %copy.33), calls=%async_computation.4 | async-start | bytes 4194304 | tf_op jit(solution)/shard_map/all_to_all | solution.py:163
  670.6 2.5 copy-start.1
Sparse Core Ops, SparseCore 0:
  8.9 37.0 all-gather.4
  50.8 45.2 all-gather.6
  97.7 26.9 all-gather.8
  126.0 21.6 all-gather.10

commit v2 on v1

--- a/solution.py
+++ b/solution.py
@@ -96,6 +96,140 @@
     )(q_t, k_all, v_all)
 
 
+MESH_ID = pl.DeviceIdType.MESH
+
+
+def flip_bits(index, pattern, n_bits):
+    result = 0
+    for bit in range(n_bits):
+        digit = (index // (1 << bit)) % 2
+        result = result + ((1 - digit) if (pattern >> bit) & 1 else digit) * (1 << bit)
+    return result
+
+
+def expert_kernel(n_chips, order, rounds, h_ref, gate_a, gate_b, up_a, up_b, down_a, down_b, z_ref,
+                  recv, w_gate, w_up, w_down, act, total, z_out, load_sem, own_sem, send_sem, recv_sem, back_sem, home_sem):
+    n_bits = n_chips.bit_length() - 1
+    dp_index = lax.axis_index("dp")
+    cp_index = lax.axis_index("cp")
+    tp_index = lax.axis_index("tp")
+    core = tp_index % 2
+    chip = cp_index * 2 + tp_index // 2
+
+    def peer(pattern):
+        other = flip_bits(chip, pattern, n_bits)
+        return (dp_index, other // 2, (other % 2) * 2 + core)
+
+    loads = []
+    for half, refs in enumerate(((gate_a, up_a, down_a), (gate_b, up_b, down_b))):
+        for which, (src, dst) in enumerate(zip(refs, (w_gate, w_up, w_down))):
+            loads.append(pltpu.make_async_copy(src.at[0], dst.at[half], load_sem.at[half, which]))
+    for load in loads:
+        load.start()
+    own = pltpu.make_async_copy(h_ref.at[0], recv.at[0], own_sem.at[0])
+    own.start()
+
+    barrier = pltpu.get_barrier_semaphore()
+    for pattern in range(1, n_chips):
+        pl.semaphore_signal(barrier, inc=1, device_id=peer(pattern), device_id_type=MESH_ID)
+    pl.semaphore_wait(barrier, n_chips - 1)
+
+    sends = {}
+    for pattern in order:
+        sends[pattern] = pltpu.make_async_remote_copy(
+            src_ref=h_ref.at[pattern], dst_ref=recv.at[pattern], send_sem=send_sem.at[pattern], recv_sem=recv_sem.at[pattern],
+            device_id=peer(pattern), device_id_type=MESH_ID)
+        sends[pattern].start()
+
+    rows = recv.shape[1]
+    hid = recv.shape[2]
+    ffn = w_gate.shape[2]
+    tile = 256
+    backs = {}
+    own.wait()
+    for turn, (first, second) in enumerate(rounds):
+        for pattern in (first, second):
+            if pattern:
+                sends[pattern].wait_recv()
+        for half in range(2):
+            if turn == 0:
+                loads[half * 3].wait()
+                loads[half * 3 + 1].wait()
+
+        x_blk = jnp.concatenate([recv[first], recv[second]], axis=0)
+
+        def half_step(half, carry):
+            for col in range(0, ffn, tile):
+                gate_pre = jnp.dot(x_blk, w_gate[half, :, col:col + tile], preferred_element_type=jnp.float32)
+                up_pre = jnp.dot(x_blk, w_up[half, :, col:col + tile], preferred_element_type=jnp.float32)
+                act[half, :, col:col + tile] = (jax.nn.silu(gate_pre) * up_pre).astype(jnp.bfloat16)
+            return carry
+
+        lax.fori_loop(0, 2, half_step, 0)
+        if turn == 0:
+            for half in range(2):
+                loads[half * 3 + 2].wait()
+
+        def out_step(col, carry):
+            at = pl.multiple_of(col * tile, tile)
+            z_blk = jnp.dot(act[0], w_down[0, :, pl.ds(at, tile)], preferred_element_type=jnp.float32)
+            z_blk = z_blk + jnp.dot(act[1], w_down[1, :, pl.ds(at, tile)], preferred_element_type=jnp.float32)
+            z_blk = z_blk.astype(jnp.bfloat16)
+            z_out[first, :, pl.ds(at, tile)] = z_blk[:rows]
+            z_out[second, :, pl.ds(at, tile)] = z_blk[rows:]
+            return carry
+
+        lax.fori_loop(0, hid // tile, out_step, 0)
+        for pattern in (first, second):
+            if pattern:
+                backs[pattern] = pltpu.make_async_remote_copy(
+                    src_ref=z_out.at[pattern], dst_ref=z_ref.at[pattern], send_sem=back_sem.at[pattern], recv_sem=home_sem.at[pattern],
+                    device_id=peer(pattern), device_id_type=MESH_ID)
+            else:
+                backs[pattern] = pltpu.make_async_copy(z_out.at[pattern], z_ref.at[pattern], own_sem.at[1])
+            backs[pattern].start()
+    for pattern in order:
+        sends[pattern].wait_send()
+    for pattern in range(n_chips):
+        backs[pattern].wait()
+
+
+def expert_layer(send_buf, own_weights, other_weights):
+    n_chips, rows, hid = send_buf.shape
+    ffn = own_weights[0].shape[2]
+    order = (1, 4, 6, 5, 7, 2, 3)
+    rounds = ((0, 1), (4, 6), (5, 7), (2, 3))
+    weights = []
+    for own, other in zip(own_weights, other_weights):
+        weights += [own, other]
+    any_spec = pl.BlockSpec(memory_space=pl.ANY)
+    flops = 2 * 3 * n_chips * rows * hid * 2 * ffn
+    return pl.pallas_call(
+        functools.partial(expert_kernel, n_chips, order, rounds),
+        out_shape=jax.ShapeDtypeStruct((n_chips, rows, hid), jnp.bfloat16),
+        in_specs=[any_spec] * 7,
+        out_specs=any_spec,
+        scratch_shapes=[
+            pltpu.VMEM((n_chips, rows, hid), jnp.bfloat16),
+            pltpu.VMEM((2, hid, ffn), jnp.bfloat16),
+            pltpu.VMEM((2, hid, ffn), jnp.bfloat16),
+            pltpu.VMEM((2, ffn, hid), jnp.bfloat16),
+            pltpu.VMEM((2, 2 * rows, ffn), jnp.bfloat16),
+            pltpu.VMEM((8, 128), jnp.float32),
+            pltpu.VMEM((n_chips, rows, hid), jnp.bfloat16),
+            pltpu.SemaphoreType.DMA((2, 3)),
+            pltpu.SemaphoreType.DMA((2,)),
+            pltpu.SemaphoreType.DMA((n_chips,)),
+            pltpu.SemaphoreType.DMA((n_chips,)),
+            pltpu.SemaphoreType.DMA((n_chips,)),
+            pltpu.SemaphoreType.DMA((n_chips,)),
+        ],
+        compiler_params=pltpu.CompilerParams(collective_id=1, has_side_effects=True, vmem_limit_bytes=58 * 1024 * 1024),
+        cost_estimate=pl.CostEstimate(flops=flops, bytes_accessed=32 * 1024 * 1024, transcendentals=n_chips * rows * 2 * ffn),
+        name="expert_layer",
+    )(send_buf, *weights)
+
+
 def solution(mesh):
     n_cp = mesh.shape["cp"]
     n_tp = mesh.shape["tp"]
@@ -113,15 +247,17 @@
         local_exp = w_gate.shape[0]
         n_experts = local_exp * n_cp * n_tp // 2
         capacity = top_k * tok_dev // n_experts
-        half_hid = hid_dim // 2
-        tp_index = lax.axis_index("tp")
+        chip = lax.axis_index("cp") * 2 + lax.axis_index("tp") // 2
         n_slots = n_experts * capacity
+
+        pair_perm = [(dev_idx, dev_idx ^ 1) for dev_idx in range(n_tp)]
+        other_weights = [lax.ppermute(one, "tp", pair_perm) for one in (w_gate, w_up, w_down)]
 
         choice_hot = (ids_loc[:, :, None] == jnp.arange(n_experts)[None, None, :])
         token_hot = jnp.sum(choice_hot.astype(jnp.bfloat16), axis=1)
         earlier = (lax.broadcasted_iota(jnp.int32, (tok_dev, tok_dev), 0) > lax.broadcasted_iota(jnp.int32, (tok_dev, tok_dev), 1)).astype(jnp.bfloat16)
         rank_in = jnp.dot(earlier, token_hot, preferred_element_type=jnp.float32).astype(jnp.int32)
-        place = rank_in + jnp.arange(n_experts, dtype=jnp.int32)[None, :] * capacity
+        place = rank_in + (jnp.arange(n_experts, dtype=jnp.int32) ^ chip)[None, :] * capacity
         dest_idx = jnp.sum(jnp.where(choice_hot, place[:, None, :], 0), axis=2)
 
         x_half = lax.all_gather(x_loc, "tp", axis=0, tiled=True)
@@ -143,25 +279,7 @@
         slots = jnp.arange(n_slots, dtype=jnp.int32)
         pick = (slots[:, None] == dest_idx[:, 0][None, :]) | (slots[:, None] == dest_idx[:, 1][None, :])
         send_buf = jnp.dot(pick.astype(jnp.bfloat16), h_loc, preferred_element_type=jnp.float32).astype(jnp.bfloat16)
-        send_buf = send_buf.reshape(n_cp, n_tp // 2, 1, local_exp, capacity, hid_dim)
-        send_buf = jnp.broadcast_to(send_buf, (n_cp, n_tp // 2, 2, local_exp, capacity, hid_dim)).reshape(n_cp, n_tp, local_exp, capacity, hid_dim)
-        recv_buf = lax.all_to_all(send_buf, "tp", 1, 1, tiled=True)
-        recv_buf = lax.all_to_all(recv_buf, "cp", 0, 0, tiled=True)
-
-        gate_pre = jnp.einsum("uvech,ehf->uvecf", recv_buf, w_gate, preferred_element_type=jnp.float32)
-        up_pre = jnp.einsum("uvech,ehf->uvecf", recv_buf, w_up, preferred_element_type=jnp.float32)
-        hidden = (jax.nn.silu(gate_pre) * up_pre).astype(jnp.bfloat16)
-        z_part = jnp.einsum("uvecf,efh->uvech", hidden, w_down, preferred_element_type=jnp.float32)
-
-        my_half = tp_index % 2
-        keep_part = lax.dynamic_slice_in_dim(z_part, my_half * half_hid, half_hid, axis=4)
-        send_part = lax.dynamic_slice_in_dim(z_part, (1 - my_half) * half_hid, half_hid, axis=4)
-        pair_perm = [(dev_idx, dev_idx ^ 1) for dev_idx in range(n_tp)]
-        z_half = (keep_part + lax.ppermute(send_part, "tp", pair_perm)).astype(jnp.bfloat16)
-
-        back_buf = lax.all_to_all(z_half, "cp", 0, 0, tiled=True)
-        back_buf = lax.all_to_all(back_buf, "tp", 1, 1, tiled=True)
-        z_full = back_buf.reshape(n_cp, n_tp // 2, 2, local_exp, capacity, half_hid).transpose(0, 1, 3, 4, 2, 5).reshape(n_slots, hid_dim)
+        z_full = expert_layer(send_buf.reshape(n_experts, capacity, hid_dim), (w_gate, w_up, w_down), other_weights).reshape(n_slots, hid_dim)
         y_loc = h_loc.astype(jnp.float32)
         for choice in range(top_k):
             take = (dest_idx[:, choice][:, None] == slots[None, :]).astype(jnp.bfloat16)

time: 680 us -> 486 us (0.71)
  waiting for transfers between devices: 244 us -> 118 us
  blocking collectives: 106 us -> 0 us
  Pallas kernels: 226 us -> 321 us
  matrix products: 57 us -> 22.4 us
  local copies, waits for them, and re-layouts: 16.6 us -> 6.34 us
  starting transfers between devices: 12.5 us -> 4.64 us
    all_to_all x2 -> x0, waiting for transfers between devices: 118 us -> none  [the longest x1 92.7 us: device_step(): recv_buf = lax.all_to_all(recv_buf, 'cp', 0, 0, tiled=True)]
    all_to_all x2 -> x0, blocking collectives: 106 us -> none  [the longest x1 55.5 us: device_step(): back_buf = lax.all_to_all(z_half, 'cp', 0, 0, tiled=True)]
    pallas_call x0 -> x1, Pallas kernels: none -> 95 us  [expert_layer(): pl.pallas_call(functools.partial(expert_kernel, n_chips, order, rounds),...]
    dot_general x2 -> x0, matrix products: 37.5 us -> none  [the longest x1 23.9 us: device_step(): jnp.einsum('uvecf,efh->uvech', hidden, w_down, preferred_element_type=jnp...]
    all_to_all x2 -> x0, starting transfers between devices: 8.66 us -> none  [the longest x1 4.84 us: device_step(): recv_buf = lax.all_to_all(recv_buf, 'cp', 0, 0, tiled=True)]
    ppermute x1 -> x3, waiting for transfers between devices: 7.1 us -> 0.01 us  [device_step(): lax.ppermute(one, 'tp', pair_perm)]
  transfers between devices with their start and end apart: 8 -> 8, of which waited for: 7 -> 4; matrix products, arithmetic and copies ran while one was open for 2% -> 3% of each run, Pallas kernels for 33% -> 46%
where the time goes in v2:
time: 486 us
  Pallas kernels  321 us (66%)
  waiting for transfers between devices  118 us (24%)
  matrix products  22.4 us (5%)
  between operations  13.4 us (3%)
  local copies, waits for them, and re-layouts  6.34 us (1%)
    pallas_call x1, Pallas kernels, attention(): pl.pallas_call(functools.partial(attn_kernel, n_cp, chunk, bq, bk, heads,...  226 us
    pallas_call x1, Pallas kernels, expert_layer(): pl.pallas_call(functools.partial(expert_kernel, n_chips, order, rounds),...  95 us
    all_gather x1, waiting for transfers between devices, device_step(): x_half = lax.all_gather(x_loc, 'tp', axis=0, tiled=True)  38.7 us
    all_gather x1, waiting for transfers between devices, device_step(): k_all = lax.all_gather(k_cur, 'cp', axis=0, tiled=True)  36.2 us
    all_gather x1, waiting for transfers between devices, device_step(): v_all = lax.all_gather(v_cur, 'cp', axis=1, tiled=True)  28.6 us
    all_to_all x1, waiting for transfers between devices, device_step(): lax.all_to_all(out_t, 'tp', 1, 0, tiled=True)  13.7 us
  transfers between devices with their start and end apart: 8, of which 4 were waited for; matrix products, arithmetic and copies ran while one was open for 3% of the time, Pallas kernels for 46%

profile of v2, /device:TPU:0, one launch (start us, length us, event | category | flops | bytes accessed | tf_op | source)
XLA Modules:
  0.0 485.7 jit_solution(8697971370934428660)
XLA Ops:
  6.5 0.0 copy-start
  6.5 0.0 all-gather.5.cloned.1.call-start
  6.5 0.7 all-gather.5.cloned.1.call-update
  7.3 0.0 all-gather.7.cloned.1.call-start
  7.3 38.7 %all-gather.5.cloned.1.call-done = bf16[2048,1024]{1,0:T(8,128)(2,1)} async-done(((bf16[512,1024]{1,0:T(8,128)(2,1)}), bf16[2048,1024]{1,0:T(8,128)(2,1)}) %all-gather.5.cloned.1.call-update) | async-done | bytes 4194320 | tf_op jit(solution)/shard_map/all_gather | solution.py:263
  46.0 3.6 fusion.31
  49.5 0.0 copy-start.4
  49.6 1.0 copy.18
  50.6 0.0 all-gather.7.cloned.1.call-update
  50.6 0.0 copy-start.5
  50.6 0.0 all-gather.9.cloned.1.call-start
  50.7 0.0 copy-done.4
  50.7 4.3 fusion.9
  55.0 0.0 all-gather.9.cloned.1.call-update
  55.0 0.0 all-gather.11.cloned.1.call-start
  55.1 0.3 collective-permute-start
  55.4 0.3 collective-permute-start.1
  55.6 0.2 collective-permute-start.2
  55.9 0.0 all-gather.11.cloned.1.call-update
  55.9 0.0 copy-done.5
  55.9 0.0 copy-done
  56.0 3.5 fusion.6
  59.4 0.1 fusion.28
  59.5 0.3 fusion.12.q_ref
  59.8 36.2 %all-gather.7.cloned.1.call-done.k_ref = bf16[8192,64]{1,0:T(8,128)(2,1)} async-done(((bf16[2048,64]{1,0:T(8,128)(2,1)}), bf16[8192,64]{1,0:T(8,128)(2,1)}) %all-gather.7.cloned.1.call-update) | async-done | bytes 1048592 | tf_op jit(solution)/shard_map/all_gather | solution.py:270
  96.0 28.6 %all-gather.9.cloned.1.call-done.v_ref = bf16[64,8192]{1,0:T(8,128)(2,1)} async-done(((bf16[64,2048]{1,0:T(8,128)(2,1)}), bf16[64,8192]{1,0:T(8,128)(2,1)}) %all-gather.9.cloned.1.call-update) | async-done | bytes 1048592 | tf_op jit(solution)/shard_map/all_gather | solution.py:271
  124.6 0.0 copy-start.2
  124.6 1.2 copy-done.2
  125.8 225.6 %causal_attention.1 = bf16[8,32,2048]{2,1,0:T(8,128)(2,1)S(1)} custom-call(bf16[8,64,2048]{2,1,0:T(8,128)(2,1)S(1)} %fusion.12.q_ref, bf16[8192,64]{1,0:T(8,128)(2,1)} %all-gather.7.cloned.1.call-done.k_ref, bf16[64,8192]{1,0:T(8,128)(2,1)S(1)} %copy-done.2), custom_call_target="tpu_custom_call" | custom-call | flops 17179869184 | bytes 8388608 | tf_op jit(solution)/shard_map/causal_attention/pallas_call | solution.py:78
  351.4 0.0 copy-start.1
  351.4 1.0 copy-done.1
  352.4 1.8 reshape.39
  354.2 0.0 copy-start.6
  354.2 0.0 copy-start.3
  354.3 1.2 copy.19
  355.4 3.7 all-to-all-start
  359.1 0.2 fusion.21
  359.4 0.1 select_reduce_fusion
  359.4 0.0 copy-done.6
  359.4 0.0 all-gather.11.cloned.1.call-done
  359.5 13.7 %all-to-all-done = bf16[256,4,512]{2,0,1:T(8,128)(2,1)S(1)} async-done(((bf16[256,4,512]{2,0,1:T(8,128)(2,1)}), bf16[256,4,512]{2,0,1:T(8,128)(2,1)S(1)}, u32[]{:S(2)}, u32[]{:S(2)}) %all-to-all-start) | async-done | bytes 1048608 | tf_op jit(solution)/shard_map/all_to_all | solution.py:274
  373.1 0.0 copy-done.3
  373.1 2.9 add_convert_fusion.1
  376.0 2.6 fusion.18
  378.6 0.0 collective-permute-done.gate_b
  378.6 0.0 collective-permute-done.1.up_b
  378.6 0.0 collective-permute-done.2.down_b
  378.6 95.0 %expert_layer.1 = bf16[8,128,1024]{2,1,0:T(8,128)(2,1)} custom-call(bf16[8,128,1024]{2,1,0:T(8,128)(2,1)} %bitcast.47, bf16[1,1024,1792]{2,1,0:T(8,128)(2,1)} %gate_a.1, bf16[1,1024,1792]{2,1,0:T(8,128)(2,1)} %collective-permute-done.gate_b, bf16[1,1024,1792]{2,1,0:T(8,128)(2,1)} %up_a.1, bf16[1,1024,1792]{2,1,0:T(8,128)(2,1)} %collective-permute-done.1.up_b, ...), custom_call_target="tpu_custom_call" | custom-call | flops 22548578304 | bytes 33554432 | tf_op jit(solution)/shard_map/expert_layer/pallas_call | solution.py:207
  473.7 0.0 copy-start.7
  473.7 3.0 fusion.13
  476.7 0.0 copy-done.7
  476.7 2.4 add_convert_fusion
  (5 shorter events, 0.1 us)
Async XLA Ops:
  6.5 49.4 %copy-start = (bf16[1024,8,32]{0,2,1:T(8,128)(2,1)S(1)}, bf16[1024,8,32]{0,2,1:T(8,128)(2,1)}, u32[]{:S(2)}) copy-start(bf16[1024,8,32]{0,2,1:T(8,128)(2,1)} %param.11) | copy-start | bytes 1572868
  6.5 39.4 %all-gather.5.cloned.1.call-start = ((), (), s32[]{:S(2)}) async-start(), calls=%async_computation.1 | async-start | bytes 5242880 | tf_op jit(solution)/shard_map/all_gather | solution.py:263
  7.3 88.8 %all-gather.7.cloned.1.call-start = ((), (), s32[]{:S(2)}) async-start(), calls=%async_computation.2 | async-start | bytes 2621440 | tf_op jit(solution)/shard_map/all_gather | solution.py:270
  49.5 1.1 copy-start.4
  50.6 5.3 %copy-start.5 = (s32[512,2]{0,1:T(2,128)S(1)}, s32[512,2]{0,1:T(2,128)}, u32[]{:S(2)}) copy-start(s32[512,2]{0,1:T(2,128)} %param.15) | copy-start | bytes 12292
  50.6 74.0 %all-gather.9.cloned.1.call-start = ((), (), s32[]{:S(2)}) async-start(), calls=%async_computation.3 | async-start | bytes 1310720 | tf_op jit(solution)/shard_map/all_gather | solution.py:271
  55.0 304.5 %all-gather.11.cloned.1.call-start = ((), (), s32[]{:S(2)}) async-start(), calls=%async_computation.4 | async-start | bytes 2621440 | tf_op jit(solution)/shard_map/all_gather | solution.py:275
  55.1 323.5 %collective-permute-start = (bf16[1,1024,1792]{2,1,0:T(8,128)(2,1)}, bf16[1,1024,1792]{2,1,0:T(8,128)(2,1)}, u32[]{:S(2)}, u32[]{:S(2)}) collective-permute-start(bf16[1,1024,1792]{2,1,0:T(8,128)(2,1)} %gate_a.1), channel_id=1, source_target_pairs={{0,1},{1,0},{2,3},{3,2},{4,5},{5,4},{6,7},{7,6},{8,9},{9,8},{10,11... | collective-permute-start | bytes 11010056 | tf_op jit(solution)/shard_map/ppermute | solution.py:254
  55.4 323.2 %collective-permute-start.1 = (bf16[1,1024,1792]{2,1,0:T(8,128)(2,1)}, bf16[1,1024,1792]{2,1,0:T(8,128)(2,1)}, u32[]{:S(2)}, u32[]{:S(2)}) collective-permute-start(bf16[1,1024,1792]{2,1,0:T(8,128)(2,1)} %up_a.1), channel_id=1, source_target_pairs={{0,1},{1,0},{2,3},{3,2},{4,5},{5,4},{6,7},{7,6},{8,9},{9,8},{10,11... | collective-permute-start | bytes 11010056 | tf_op jit(solution)/shard_map/ppermute | solution.py:254
  55.6 323.0 %collective-permute-start.2 = (bf16[1,1792,1024]{2,1,0:T(8,128)(2,1)}, bf16[1,1792,1024]{2,1,0:T(8,128)(2,1)}, u32[]{:S(2)}, u32[]{:S(2)}) collective-permute-start(bf16[1,1792,1024]{2,1,0:T(8,128)(2,1)} %down_a.1), channel_id=1, source_target_pairs={{0,1},{1,0},{2,3},{3,2},{4,5},{5,4},{6,7},{7,6},{8,9},{9,8},{10,11... | collective-permute-start | bytes 11010056 | tf_op jit(solution)/shard_map/ppermute | solution.py:254
  124.6 1.2 copy-start.2
  351.4 1.0 copy-start.1
  354.2 5.2 %copy-start.6 = (f32[512,2]{0,1:T(2,128)S(1)}, f32[512,2]{0,1:T(2,128)}, u32[]{:S(2)}) copy-start(f32[512,2]{0,1:T(2,128)} %param.16) | copy-start | bytes 12292
  354.2 18.9 %copy-start.3 = (bf16[512,1024]{1,0:T(8,128)(2,1)S(1)}, bf16[512,1024]{1,0:T(8,128)(2,1)}, u32[]{:S(2)}) copy-start(bf16[512,1024]{1,0:T(8,128)(2,1)} %param.10) | copy-start | bytes 3145732
  355.4 17.7 %all-to-all-start = ((bf16[256,4,512]{2,0,1:T(8,128)(2,1)}), bf16[256,4,512]{2,0,1:T(8,128)(2,1)S(1)}, u32[]{:S(2)}, u32[]{:S(2)}) async-start(bf16[256,4,512]{2,0,1:T(8,128)(2,1)} %copy.19), calls=%async_computation | async-start | bytes 2097152 | tf_op jit(solution)/shard_map/all_to_all | solution.py:274
  473.7 3.1 copy-start.7
Sparse Core Ops, SparseCore 0:
  8.9 37.0 all-gather.4
  50.7 45.2 all-gather.6
  97.6 26.9 all-gather.8
  126.0 21.6 all-gather.10

commit v3 on v2

--- a/solution.py
+++ b/solution.py
@@ -9,94 +9,322 @@
 from jax.sharding import PartitionSpec as P
 
 
-def attn_kernel(n_cp, chunk, bq, bk, heads, grp, q_ref, k_ref, v_ref, o_ref, m_ref, l_ref, acc_ref):
-    head_dim = acc_ref.shape[1]
+MESH_ID = pl.DeviceIdType.MESH
+
+
+def project_kernel(pieces, x_ref, w_q_ref, w_k_ref, w_v_ref, q_ref, k_ref, v_ref, x_all, k_dup, pair_send, pair_recv, far_send, far_recv, pass_send, pass_recv):
+    dp_index = lax.axis_index("dp")
     cp_index = lax.axis_index("cp")
-    step = pl.program_id(0)
-    q_per = chunk // bq
-    k_per = chunk // bk
-    half = step // q_per
-    in_chunk = step % q_per
-    my_chunk = jnp.where(half == 0, cp_index, 2 * n_cp - 1 - cp_index)
-    diag = (in_chunk * bq) // bk
+    me = lax.axis_index("tp")
+    pair = me + 1 - 2 * (me % 2)
+    far = (me + 2) % 4
+    far_pair = (pair + 2) % 4
+    tok = x_ref.shape[0]
+    rows = tok // pieces
+
+    barrier = pltpu.get_barrier_semaphore()
+    for other in (pair, far):
+        pl.semaphore_signal(barrier, inc=1, device_id=(dp_index, cp_index, other), device_id_type=MESH_ID)
+    pl.semaphore_wait(barrier, 2)
+
+    def piece(ref, num):
+        return ref.at[pl.ds(num * rows, rows)]
+
+    far_copies, pass_copies = [], []
+    for num in range(pieces):
+        far_copies.append(pltpu.make_async_remote_copy(
+            src_ref=piece(x_ref, num), dst_ref=x_all.at[me, pl.ds(num * rows, rows)], send_sem=far_send.at[num], recv_sem=far_recv.at[num],
+            device_id=(dp_index, cp_index, far), device_id_type=MESH_ID))
+        far_copies[num].start()
+        pass_copies.append(pltpu.make_async_remote_copy(
+            src_ref=x_all.at[far, pl.ds(num * rows, rows)], dst_ref=x_all.at[far, pl.ds(num * rows, rows)], send_sem=pass_send.at[num], recv_sem=pass_recv.at[num],
+            device_id=(dp_index, cp_index, pair), device_id_type=MESH_ID))
+    pair_copy = pltpu.make_async_remote_copy(
+        src_ref=x_ref, dst_ref=x_all.at[me], send_sem=pair_send.at[0], recv_sem=pair_recv.at[0],
+        device_id=(dp_index, cp_index, pair), device_id_type=MESH_ID)
+    pair_copy.start()
+
+    contract = (((1,), (1,)), ((), ()))
+
+    def project(x_blk, block, start, size):
+        q_ref[block, :, start:start + size] = lax.dot_general(w_q_ref[...], x_blk, contract, preferred_element_type=jnp.float32).astype(jnp.bfloat16)
+        v_ref[block, :, start:start + size] = lax.dot_general(w_v_ref[...], x_blk, contract, preferred_element_type=jnp.float32).astype(jnp.bfloat16)
+        w_k = w_k_ref[...]
+        k_blk = lax.dot_general(x_blk, jnp.concatenate([w_k, w_k], axis=0), contract, preferred_element_type=jnp.float32)
+        k_dup[block, start:start + size, :] = k_blk.astype(jnp.bfloat16)
+
+    project(x_ref[...], me, 0, tok)
+    pair_copy.wait_recv()
+    project(x_all[pair], pair, 0, tok)
+    for num in range(pieces):
+        far_copies[num].wait_recv()
+        pass_copies[num].start()
+        project(x_all[far, num * rows:(num + 1) * rows], far, num * rows, rows)
+        pass_copies[num].wait_recv()
+        project(x_all[far_pair, num * rows:(num + 1) * rows], far_pair, num * rows, rows)
+    low = lax.broadcasted_iota(jnp.int32, k_dup.shape[1:], 1) < k_dup.shape[2] // 2
+    for half in range(2):
+        k_ref[half] = jnp.where(low, k_dup[2 * half].astype(jnp.float32), k_dup[2 * half + 1].astype(jnp.float32)).astype(jnp.bfloat16)
+    pair_copy.wait_send()
+    for num in range(pieces):
+        far_copies[num].wait_send()
+        pass_copies[num].wait_send()
+
+
+def project_rows(x_loc, w_q, w_k, w_v, n_tp):
+    tok, hid = x_loc.shape
+    pieces = 4
+    depth_q = w_q.shape[0]
+    depth_k = w_k.shape[0]
+    vmem = pl.BlockSpec(memory_space=pltpu.VMEM)
+    return pl.pallas_call(
+        functools.partial(project_kernel, pieces),
+        out_shape=(
+            jax.ShapeDtypeStruct((n_tp, depth_q, tok), jnp.bfloat16),
+            jax.ShapeDtypeStruct((n_tp // 2, tok, 2 * depth_k), jnp.bfloat16),
+            jax.ShapeDtypeStruct((n_tp, depth_k, tok), jnp.bfloat16),
+        ),
+        in_specs=[vmem] * 4,
+        out_specs=(vmem, vmem, vmem),
+        scratch_shapes=[
+            pltpu.VMEM((n_tp, tok, hid), jnp.bfloat16),
+            pltpu.VMEM((n_tp, tok, 2 * depth_k), jnp.bfloat16),
+            pltpu.SemaphoreType.DMA((1,)),
+            pltpu.SemaphoreType.DMA((1,)),
+            pltpu.SemaphoreType.DMA((pieces,)),
+            pltpu.SemaphoreType.DMA((pieces,)),
+            pltpu.SemaphoreType.DMA((pieces,)),
+            pltpu.SemaphoreType.DMA((pieces,)),
+        ],
+        compiler_params=pltpu.CompilerParams(collective_id=0, has_side_effects=True, vmem_limit_bytes=40 * 1024 * 1024),
+        cost_estimate=pl.CostEstimate(flops=2 * n_tp * tok * hid * (depth_q + 2 * depth_k), bytes_accessed=8 * 1024 * 1024, transcendentals=0),
+        name="project_rows",
+    )(x_loc, w_q, w_k, w_v)
+
+
+def attn_kernel(n_cp, n_tp, heads, grp, head_dim, q_ref, kc_ref, vc_ref, w_o_ref, gate_ref, up_ref, down_ref,
+                o_ref, w_o_all, gate_other, up_other, down_other,
+                q3_ref, kc_all, v_all, k_exp, m_ref, old_ref, l_ref, acc_ref, s0_ref, s1_ref, o_send,
+                k_send, k_recv, v_send, v_recv, local_sem, wo_send, wo_recv, ex_send, ex_recv, out_send, out_recv):
+    dp_index = lax.axis_index("dp")
+    me = lax.axis_index("cp")
+    tp_index = lax.axis_index("tp")
+    blk = q_ref.shape[2]
+    kv_heads = heads // grp
+    depth = k_exp.shape[2] // kv_heads
     score_scale = head_dim ** -0.5 * math.log2(math.e)
-
-    def key_offset(blk):
-        chunk_id = blk // k_per
-        rank = jnp.where(chunk_id < n_cp, chunk_id, 2 * n_cp - 1 - chunk_id)
-        upper = jnp.where(chunk_id < n_cp, 0, 1)
-        return rank * (2 * chunk) + upper * chunk + (blk % k_per) * bk
-
-    def visit(blk, first):
-        off = pl.multiple_of(key_offset(blk), bk)
-        k_blk = k_ref[pl.ds(off, bk), :]
-        v_blk = v_ref[:, pl.ds(off, bk)]
-        if first:
-            k_pos = diag * bk + lax.broadcasted_iota(jnp.int32, (bk, bq), 0)
-            q_pos = in_chunk * bq + lax.broadcasted_iota(jnp.int32, (bk, bq), 1)
-            allowed = k_pos <= q_pos
+    s_refs = (s0_ref, s1_ref)
+    near = me + 1 - 2 * (me % 2)
+    mid = 2 - me // 2
+    end = 3 * (1 - me // 2)
+    others = (near, mid, end)
+
+    def cp_peer(rank):
+        return (dp_index, rank, tp_index)
+
+    def tp_peer(rank):
+        return (dp_index, me, rank)
+
+    barrier = pltpu.get_barrier_semaphore()
+    for rank in others:
+        pl.semaphore_signal(barrier, inc=1, device_id=cp_peer(rank), device_id_type=MESH_ID)
+    for shift in range(1, n_tp):
+        pl.semaphore_signal(barrier, inc=1, device_id=tp_peer((tp_index + shift) % n_tp), device_id_type=MESH_ID)
+    pl.semaphore_wait(barrier, n_cp - 1 + n_tp - 1)
+
+    def key_copies(step, half, rank, owner):
+        k_copy = pltpu.make_async_remote_copy(
+            src_ref=kc_ref.at[half], dst_ref=kc_all.at[owner * 2 + half], send_sem=k_send.at[step, half], recv_sem=k_recv.at[owner, half],
+            device_id=cp_peer(rank), device_id_type=MESH_ID)
+        v_copy = pltpu.make_async_remote_copy(
+            src_ref=vc_ref.at[pl.ds(half * 2, 2)], dst_ref=v_all.at[pl.ds((owner * 2 + half) * 2, 2)], send_sem=v_send.at[step, half], recv_sem=v_recv.at[owner, half],
+            device_id=cp_peer(rank), device_id_type=MESH_ID)
+        return k_copy, v_copy
+
+    for step, rank in enumerate(others):
+        for copy in key_copies(step, 0, rank, me):
+            copy.start()
+
+        @pl.when(rank < me)
+        def _():
+            for copy in key_copies(step, 1, rank, me):
+                copy.start()
+
+    wo_copies = [pltpu.make_async_copy(w_o_ref, w_o_all.at[0], local_sem.at[0])]
+    for shift in range(1, n_tp):
+        wo_copies.append(pltpu.make_async_remote_copy(
+            src_ref=w_o_ref, dst_ref=w_o_all.at[shift], send_sem=wo_send.at[shift], recv_sem=wo_recv.at[shift],
+            device_id=tp_peer((tp_index + shift) % n_tp), device_id_type=MESH_ID))
+    pair = tp_index + 1 - 2 * (tp_index % 2)
+    ex_copies = []
+    for which, (src, dst) in enumerate(((gate_ref, gate_other), (up_ref, up_other), (down_ref, down_other))):
+        ex_copies.append(pltpu.make_async_remote_copy(
+            src_ref=src, dst_ref=dst, send_sem=ex_send.at[which], recv_sem=ex_recv.at[which], device_id=tp_peer(pair), device_id_type=MESH_ID))
+    for copy in wo_copies + ex_copies:
+        copy.start()
+
+    for block in range(n_tp):
         for head in range(heads):
-            kv = head // grp
-            scores = jnp.dot(k_blk, q_ref[head], preferred_element_type=jnp.float32)
-            if first:
-                scores = jnp.where(allowed, scores, -1e30)
-            top = jnp.max(scores, axis=0, keepdims=True)
-            if not first:
-                old = m_ref[head]
-                top = jnp.maximum(old, top)
-            prob = jnp.exp2((scores - top) * score_scale)
-            part = jnp.sum(prob.reshape(bk // 8, 8, bq), axis=0)
-            mixed = jnp.dot(v_blk[kv * head_dim:(kv + 1) * head_dim], prob.astype(jnp.bfloat16), preferred_element_type=jnp.float32)
-            m_ref[head] = top
-            if first:
-                l_ref[head] = part
-                acc_ref[head] = mixed
-            else:
-                rescale = jnp.exp2((old - top) * score_scale)
-                l_ref[head] = l_ref[head] * rescale + part
-                acc_ref[head] = acc_ref[head] * rescale + mixed
-
-    base = my_chunk * k_per
-    visit(base + diag, True)
-
-    def body(blk, carry):
-        visit(blk, False)
+            rest = q_ref[block, head * head_dim:(head + 1) * head_dim, :].astype(jnp.float32) * score_scale
+            for term in range(3):
+                part = rest.astype(jnp.bfloat16)
+                q3_ref[block, head, term * head_dim:(term + 1) * head_dim, :] = part
+                rest = rest - part.astype(jnp.float32)
+            q3_ref[block, head, 3 * head_dim:, :] = jnp.zeros((depth - 3 * head_dim, blk), jnp.bfloat16)
+    m_ref[...] = jnp.full(m_ref.shape, -1e30, jnp.float32)
+    l_ref[...] = jnp.zeros(l_ref.shape, jnp.float32)
+    acc_ref[...] = jnp.zeros(acc_ref.shape, jnp.float32)
+
+    lane = lax.broadcasted_iota(jnp.int32, (kc_ref.shape[2], k_exp.shape[2]), 0)
+    col = lax.broadcasted_iota(jnp.int32, (kc_ref.shape[2], k_exp.shape[2]), 1)
+    spread = [(lane == sub * (kv_heads * head_dim) + (col // depth) * head_dim + col % head_dim).astype(jnp.bfloat16) for sub in range(2)]
+
+    def expand(k_half, at):
+        for sub in range(2):
+            k_exp[at * 2 + sub] = jnp.dot(k_half, spread[sub], preferred_element_type=jnp.float32).astype(jnp.bfloat16)
+
+    def score(head, block, at, masked):
+        kv = head // grp
+        scores = jnp.dot(k_exp[at, :, kv * depth:(kv + 1) * depth], q3_ref[block, head], preferred_element_type=jnp.float32)
+        if masked:
+            k_pos = lax.broadcasted_iota(jnp.int32, (blk, blk), 0)
+            q_pos = lax.broadcasted_iota(jnp.int32, (blk, blk), 1)
+            scores = jnp.where(k_pos <= q_pos, scores, -1e30)
+        s_refs[head % 2][...] = scores
+        old = m_ref[block, head]
+        old_ref[head] = old
+        m_ref[block, head] = jnp.maximum(old, jnp.max(scores, axis=0, keepdims=True))
+
+    def mix(head, block, at):
+        kv = head // grp
+        top = m_ref[block, head]
+        prob = jnp.exp2(s_refs[head % 2][...] - top)
+        part = jnp.sum(prob.reshape(blk // 8, 8, blk), axis=0)
+        mixed = jnp.dot(v_all[at, kv * head_dim:(kv + 1) * head_dim, :], prob.astype(jnp.bfloat16), preferred_element_type=jnp.float32)
+        rescale = jnp.exp2(old_ref[head] - top)
+        l_ref[block, head] = l_ref[block, head] * rescale + part
+        acc_ref[block, head] = acc_ref[block, head] * rescale + mixed
+
+    def run(count, place, masked):
+        block, at = place(0)
+        score(0, block, at, masked)
+
+        def body(num, carry):
+            block, at = place(num)
+            next_block, next_at = place(num + 1 - (num + 1) // count)
+            for head in range(heads):
+                if head + 1 < heads:
+                    score(head + 1, block, at, masked)
+                else:
+                    score(0, next_block, next_at, masked)
+                mix(head, block, at)
+            return carry
+
+        lax.fori_loop(0, count, body, 0)
+
+    for half in range(2):
+        expand(kc_ref[half], me * 2 + half)
+        for sub in range(2):
+            v_all[(me * 2 + half) * 2 + sub] = vc_ref[half * 2 + sub]
+
+    def place_diag(num):
+        return num, me * 4 + num
+
+    def place_local(num):
+        late = (num + 2) // 4
+        block = (1 - late) * (1 + 2 * num) + late * (1 + num // 2)
+        half = (1 - late) * num
+        return block, me * 4 + half * 2 + late * (num % 2)
+
+    run(4, place_diag, True)
+    run(6, place_local, False)
+
+    def visit_rank(step, carry):
+        rank = ((2 - step) // 2) * near + (step % 2) * mid + (step // 2) * end
+        below = (me - rank + 3) // 4
+        for copy in key_copies(0, 0, rank, rank):
+            copy.wait_recv()
+        expand(kc_all[rank * 2], rank * 2)
+
+        @pl.when(rank > me)
+        def _():
+            for copy in key_copies(0, 1, rank, rank):
+                copy.wait_recv()
+            expand(kc_all[rank * 2 + 1], rank * 2 + 1)
+
+        def place(num):
+            block = below * (num // 2) + (1 - below) * (2 + num // 4)
+            half = (1 - below) * ((num // 2) % 2)
+            return block, rank * 4 + half * 2 + num % 2
+
+        run(8, place, False)
         return carry
 
-    lax.fori_loop(0, base + diag, body, 0)
-    for head in range(heads):
-        total = jnp.sum(l_ref[head], axis=0, keepdims=True)
-        o_ref[head] = (acc_ref[head] / total).astype(o_ref.dtype)
-
-
-def attention(q_t, k_all, v_all, n_cp, head_dim, bq=256, bk=512):
-    heads, depth, rows = q_t.shape
-    chunk = rows // 2
-    n_keys = k_all.shape[0]
-    grp = heads // (depth // head_dim)
-    pairs = heads * rows * n_keys // 2
+    lax.fori_loop(0, n_cp - 1, visit_rank, 0)
+
+    outs = []
+    for shift in (2, 1, 3, 0):
+        block = (tp_index + shift) % n_tp
+        for head in range(heads):
+            total = jnp.sum(l_ref[block, head], axis=0, keepdims=True)
+            o_send[block, head * head_dim:(head + 1) * head_dim, :] = (acc_ref[block, head] / total).astype(jnp.bfloat16)
+        if shift:
+            outs.append(pltpu.make_async_remote_copy(
+                src_ref=o_send.at[block], dst_ref=o_ref.at[shift], send_sem=out_send.at[shift], recv_sem=out_recv.at[shift],
+                device_id=tp_peer(block), device_id_type=MESH_ID))
+        else:
+            outs.append(pltpu.make_async_copy(o_send.at[block], o_ref.at[0], local_sem.at[1]))
+        outs[-1].start()
+    for step, rank in enumerate(others):
+        for copy in key_copies(step, 0, rank, me):
+            copy.wait_send()
+
+        @pl.when(rank < me)
+        def _():
+            for copy in key_copies(step, 1, rank, me):
+                copy.wait_send()
+
+    for copy in wo_copies + ex_copies + outs:
+        copy.wait()
+
+
+def attention(q_t, k_c, v_c, w_o, experts, n_cp, head_dim, kv_heads):
+    n_tp, q_depth, blk = q_t.shape
+    heads = q_depth // head_dim
+    grp = heads // kv_heads
+    hid = w_o.shape[1]
+    depth = 128
+    pairs = heads * (n_tp * blk) ** 2 * n_cp // 2
+    vmem = pl.BlockSpec(memory_space=pltpu.VMEM)
+    any_spec = pl.BlockSpec(memory_space=pl.ANY)
+    dma = pltpu.SemaphoreType.DMA
     return pl.pallas_call(
-        functools.partial(attn_kernel, n_cp, chunk, bq, bk, heads, grp),
-        out_shape=jax.ShapeDtypeStruct((heads, head_dim, rows), jnp.bfloat16),
-        grid=(rows // bq,),
-        in_specs=[
-            pl.BlockSpec((heads, depth, bq), lambda i: (0, 0, i)),
-            pl.BlockSpec((n_keys, depth), lambda i: (0, 0)),
-            pl.BlockSpec((depth, n_keys), lambda i: (0, 0)),
+        functools.partial(attn_kernel, n_cp, n_tp, heads, grp, head_dim),
+        out_shape=(
+            jax.ShapeDtypeStruct((n_tp, q_depth, blk), jnp.bfloat16),
+            jax.ShapeDtypeStruct((n_tp, q_depth, hid), jnp.bfloat16),
+        ) + tuple(jax.ShapeDtypeStruct(one.shape, one.dtype) for one in experts),
+        in_specs=[vmem] * 3 + [any_spec] * 4,
+        out_specs=(any_spec,) * 5,
+        scratch_shapes=[
+            pltpu.VMEM((n_tp, heads, depth, blk), jnp.bfloat16),
+            pltpu.VMEM((2 * n_cp,) + k_c.shape[1:], jnp.bfloat16),
+            pltpu.VMEM((4 * n_cp,) + v_c.shape[1:], jnp.bfloat16),
+            pltpu.VMEM((4 * n_cp, blk, kv_heads * depth), jnp.bfloat16),
+            pltpu.VMEM((n_tp, heads, 1, blk), jnp.float32),
+            pltpu.VMEM((heads, 1, blk), jnp.float32),
+            pltpu.VMEM((n_tp, heads, 8, blk), jnp.float32),
+            pltpu.VMEM((n_tp, heads, head_dim, blk), jnp.float32),
+            pltpu.VMEM((blk, blk), jnp.float32),
+            pltpu.VMEM((blk, blk), jnp.float32),
+            pltpu.VMEM((n_tp, q_depth, blk), jnp.bfloat16),
+            dma((n_cp - 1, 2)), dma((n_cp, 2)), dma((n_cp - 1, 2)), dma((n_cp, 2)), dma((2,)),
+            dma((n_tp,)), dma((n_tp,)), dma((3,)), dma((3,)), dma((n_tp,)), dma((n_tp,)),
         ],
-        out_specs=pl.BlockSpec((heads, head_dim, bq), lambda i: (0, 0, i)),
-        scratch_shapes=[
-            pltpu.VMEM((heads, 1, bq), jnp.float32),
-            pltpu.VMEM((heads, 8, bq), jnp.float32),
-            pltpu.VMEM((heads, head_dim, bq), jnp.float32),
-        ],
-        compiler_params=pltpu.CompilerParams(dimension_semantics=("arbitrary",), vmem_limit_bytes=48 * 1024 * 1024),
-        cost_estimate=pl.CostEstimate(flops=4 * pairs * 64, bytes_accessed=8 * 1024 * 1024, transcendentals=pairs),
+        compiler_params=pltpu.CompilerParams(collective_id=2, has_side_effects=True, vmem_limit_bytes=48 * 1024 * 1024),
+        cost_estimate=pl.CostEstimate(flops=4 * pairs * 64, bytes_accessed=40 * 1024 * 1024, transcendentals=pairs),
         name="causal_attention",
-    )(q_t, k_all, v_all)
-
-
-MESH_ID = pl.DeviceIdType.MESH
+    )(q_t, k_c, v_c, w_o, *experts)
 
 
 def flip_bits(index, pattern, n_bits):
@@ -243,15 +471,11 @@
         kv_loc = w_k.shape[1]
         heads = w_q.shape[1]
         head_dim = w_q.shape[2]
-        grp_size = heads // kv_loc
         local_exp = w_gate.shape[0]
         n_experts = local_exp * n_cp * n_tp // 2
         capacity = top_k * tok_dev // n_experts
         chip = lax.axis_index("cp") * 2 + lax.axis_index("tp") // 2
         n_slots = n_experts * capacity
-
-        pair_perm = [(dev_idx, dev_idx ^ 1) for dev_idx in range(n_tp)]
-        other_weights = [lax.ppermute(one, "tp", pair_perm) for one in (w_gate, w_up, w_down)]
 
         choice_hot = (ids_loc[:, :, None] == jnp.arange(n_experts)[None, None, :])
         token_hot = jnp.sum(choice_hot.astype(jnp.bfloat16), axis=1)
@@ -260,19 +484,10 @@
         place = rank_in + (jnp.arange(n_experts, dtype=jnp.int32) ^ chip)[None, :] * capacity
         dest_idx = jnp.sum(jnp.where(choice_hot, place[:, None, :], 0), axis=2)
 
-        x_half = lax.all_gather(x_loc, "tp", axis=0, tiled=True)
-        half_len = x_half.shape[0]
-        q_t = jnp.einsum("sh,hnd->nds", x_half, w_q, preferred_element_type=jnp.float32).astype(jnp.bfloat16)
-        q_t = q_t.reshape(kv_loc, grp_size, head_dim, half_len)
-        q_t = jnp.concatenate([jnp.pad(q_t[kv], ((0, 0), (kv * head_dim, (kv_loc - 1 - kv) * head_dim), (0, 0))) for kv in range(kv_loc)], axis=0)
-        k_cur = jnp.einsum("sh,hnd->snd", x_half, w_k, preferred_element_type=jnp.float32).astype(jnp.bfloat16).reshape(half_len, kv_loc * head_dim)
-        v_cur = jnp.einsum("sh,hnd->nds", x_half, w_v, preferred_element_type=jnp.float32).astype(jnp.bfloat16).reshape(kv_loc * head_dim, half_len)
-        k_all = lax.all_gather(k_cur, "cp", axis=0, tiled=True)
-        v_all = lax.all_gather(v_cur, "cp", axis=1, tiled=True)
-        out_t = attention(q_t, k_all, v_all, n_cp, head_dim)
-        out_t = out_t.reshape(heads * head_dim, n_tp, tok_dev)
-        out_t = lax.all_to_all(out_t, "tp", 1, 0, tiled=True).reshape(n_tp * heads * head_dim, tok_dev)
-        w_o_all = lax.all_gather(w_o.reshape(heads * head_dim, hid_dim), "tp", axis=0, tiled=True)
+        q_t, k_c, v_c = project_rows(x_loc, *(one.transpose(1, 2, 0).reshape(-1, hid_dim) for one in (w_q, w_k, w_v)), n_tp)
+        out_t, w_o_all, *other_weights = attention(q_t, k_c, v_c, w_o.reshape(heads * head_dim, hid_dim), (w_gate, w_up, w_down), n_cp, head_dim, kv_loc)
+        out_t = out_t.reshape(n_tp * heads * head_dim, tok_dev)
+        w_o_all = w_o_all.reshape(n_tp * heads * head_dim, hid_dim)
         attn_rows = lax.dot_general(out_t, w_o_all, (((0,), (0,)), ((), ())), preferred_element_type=jnp.float32)
         h_loc = (x_loc.astype(jnp.float32) + attn_rows).astype(jnp.bfloat16)
 

time: 486 us -> 243 us (0.50)
  waiting for transfers between devices: 118 us -> 0 us
  Pallas kernels: 321 us -> 227 us
  between operations: 13.4 us -> 0.12 us
  matrix products: 22.4 us -> 9.52 us
    all_gather x4 -> x0, waiting for transfers between devices: 103 us -> none  [the longest x1 38.7 us: device_step(): x_half = lax.all_gather(x_loc, 'tp', axis=0, tiled=True)]
    pallas_call x1 -> x2, Pallas kernels: 226 us -> 131 us  [the longest x1 103 us: attention(): pl.pallas_call(functools.partial(attn_kernel, n_cp, n_tp, heads, grp, hea...]
    all_to_all x1 -> x0, waiting for transfers between devices: 13.7 us -> none  [device_step(): lax.all_to_all(out_t, 'tp', 1, 0, tiled=True)]
    dot_general x2 -> x0, matrix products: 7.75 us -> none  [the longest x1 4.28 us: device_step(): jnp.einsum('sh,hnd->nds', x_half, w_v, preferred_element_type=jnp.float32)]
  transfers between devices with their start and end apart: 8 -> 0, of which waited for: 4 -> 0; matrix products, arithmetic and copies ran while one was open for 3% -> 0% of each run, Pallas kernels for 46% -> 0%
where the time goes in v3:
time: 243 us; the launch traced here: 242 us
  Pallas kernels  227 us (93%)
  matrix products  9.52 us (4%)
  local copies, waits for them, and re-layouts  4.1 us (2%)
    pallas_call x1, Pallas kernels, attention(): pl.pallas_call(functools.partial(attn_kernel, n_cp, n_tp, heads, grp, hea...  103 us
    pallas_call x1, Pallas kernels, expert_layer(): pl.pallas_call(functools.partial(expert_kernel, n_chips, order, rounds),...  96 us
    pallas_call x1, Pallas kernels, project_rows(): pl.pallas_call(functools.partial(project_kernel, pieces), out_shape=(jax....  28.5 us
    dot_general x2, matrix products, device_step(): jnp.dot(take, z_full, preferred_element_type=jnp.float32)  5.41 us

profile of v3, /device:TPU:0, one launch (start us, length us, event | category | flops | bytes accessed | tf_op | source)
XLA Modules:
  0.0 242.4 jit_solution(16195622666190530131)
XLA Ops:
  0.0 0.7 fusion.15
  0.7 0.2 fusion.9
  0.9 0.7 select_reduce_fusion
  1.7 0.0 copy-start
  1.7 1.2 copy-done
  2.9 0.0 copy-start.2
  2.9 1.0 copy-done.2
  3.9 0.0 copy-start.4
  4.0 0.9 copy-done.4
  4.9 0.0 copy-start.5
  4.9 0.9 copy-done.5
  5.8 0.0 copy-start.3
  5.8 28.5 %project_rows.1 = (bf16[4,256,512]{2,1,0:T(8,128)(2,1)S(1)}, bf16[2,512,128]{2,1,0:T(8,128)(2,1)S(1)}, bf16[4,64,512]{2,1,0:T(8,128)(2,1)S(1)}) custom-call(bf16[512,1024]{1,0:T(8,128)(2,1)S(1)} %copy-done, bf16[256,1024]{1,0:T(8,128)(2,1)S(1)} %bitcast.26, bf16[64,1024]{1,0:T(8,128)(2,1)S(1)} %bitcast.28, bf16[64,1024]{1,0:T(8,128)(2,1)S(1)} %bitcast.29), custom_call_target="tpu_custom_call" | custom-call | flops 1610612736 | bytes 8388608 | tf_op jit(solution)/shard_map/project_rows/pallas_call | solution.py:80
  34.3 0.0 copy-done.3
  34.3 0.0 copy-start.1
  34.3 102.7 %causal_attention.1 = (bf16[4,256,512]{2,1,0:T(8,128)(2,1)S(1)}, bf16[4,256,1024]{2,1,0:T(8,128)(2,1)S(1)}, bf16[1,1024,1792]{2,1,0:T(8,128)(2,1)}, bf16[1,1024,1792]{2,1,0:T(8,128)(2,1)}, bf16[1,1792,1024]{2,1,0:T(8,128)(2,1)}) custom-call(bf16[4,256,512]{2,1,0:T(8,128)(2,1)S(1)} %get-tuple-element.13.q_ref, ...), custom_call_target="tpu_custom_call" | custom-call | flops 17179869184 | bytes 41943040 | tf_op jit(solution)/shard_map/causal_attention/pallas_call | solution.py:301
  137.0 0.0 copy-done.1
  137.0 1.3 fusion
  138.2 2.6 %fusion.6 = bf16[1024,1024]{1,0:T(8,128)(2,1)} fusion(bf16[512,1024]{1,0:T(8,128)(2,1)S(1)} %fusion, s32[512]{0:T(512)S(1)} %bitcast.30, s32[512]{0:T(512)S(1)} %bitcast.32), kind=kOutput, calls=%fused_computation.11 | convolution fusion | flops 1076363264 | bytes 3149824 | tf_op jit(solution)/shard_map/dot_general | solution.py:496
  140.9 96.0 %expert_layer.1 = bf16[8,128,1024]{2,1,0:T(8,128)(2,1)} custom-call(bf16[8,128,1024]{2,1,0:T(8,128)(2,1)} %bitcast.38, bf16[1,1024,1792]{2,1,0:T(8,128)(2,1)} %gate_a.1, bf16[1,1024,1792]{2,1,0:T(8,128)(2,1)} %get-tuple-element.18.gate_b, bf16[1,1024,1792]{2,1,0:T(8,128)(2,1)} %up_a.1, bf16[1,1024,1792]{2,1,0:T(8,128)(2,1)} %get-tuple-element.19.up_b, ...), custom_call_target="tpu_custom_call" | custom-call | flops 22548578304 | bytes 33554432 | tf_op jit(solution)/shard_map/expert_layer/pallas_call | solution.py:435
  236.9 0.0 copy-start.6
  236.9 0.0 copy-start.7
  236.9 3.0 %fusion.1 = f32[512,1024]{1,0:T(8,128)S(1)} fusion(bf16[1024,1024]{1,0:T(8,128)(2,1)} %bitcast.36, s32[512]{0:T(512)S(1)} %bitcast.33), kind=kOutput, calls=%fused_computation.7 | convolution fusion | flops 1074266112 | bytes 4196352 | tf_op jit(solution)/shard_map/dot_general | solution.py:501
  239.9 0.0 copy-done.6
  240.0 0.0 copy-done.7
  240.0 2.4 add_convert_fusion
  (3 shorter events, 0.0 us)
Async XLA Ops:
  1.7 1.2 copy-start
  2.9 1.0 copy-start.2
  3.9 0.9 copy-start.4
  4.9 0.9 copy-start.5
  5.8 28.5 %copy-start.3 = (bf16[8,32,1024]{2,1,0:T(8,128)(2,1)S(1)}, bf16[8,32,1024]{2,1,0:T(8,128)(2,1)}, u32[]{:S(2)}) copy-start(bf16[8,32,1024]{2,1,0:T(8,128)(2,1)} %param.14) | copy-start | bytes 1572868
  34.3 102.7 %copy-start.1 = (bf16[512,1024]{1,0:T(8,128)(2,1)S(1)}, bf16[512,1024]{1,0:T(8,128)(2,1)}, u32[]{:S(2)}) copy-start(bf16[512,1024]{1,0:T(8,128)(2,1)} %x_ref.1) | copy-start | bytes 3145732
  236.9 3.1 %copy-start.6 = (f32[512,2]{0,1:T(2,128)S(1)}, f32[512,2]{0,1:T(2,128)}, u32[]{:S(2)}) copy-start(f32[512,2]{0,1:T(2,128)} %param.16) | copy-start | bytes 12292
  236.9 3.1 %copy-start.7 = (bf16[8,128,1024]{2,1,0:T(8,128)(2,1)S(1)}, bf16[8,128,1024]{2,1,0:T(8,128)(2,1)}, u32[]{:S(2)}) copy-start(bf16[8,128,1024]{2,1,0:T(8,128)(2,1)} %expert_layer.1) | copy-start | bytes 6291460

commit v4 on v3

v4 whole, which is shorter than its diff:
```python
import functools
import math

import jax
import jax.numpy as jnp
from jax import lax
from jax.experimental import pallas as pl
from jax.experimental.pallas import tpu as pltpu
from jax.sharding import PartitionSpec as P


MESH_ID = pl.DeviceIdType.MESH


def attn_kernel(n_cp, n_tp, heads, grp, head_dim, pieces, x_ref, w_q_ref, w_k_ref, w_v_ref, w_o_ref, gate_ref, up_ref, down_ref,
                o_ref, w_o_all, gate_other, up_other, down_other,
                x_all, w_q, w_k, w_v, k_dup, k_own, q3_ref, kc_all, v_all, k_exp, m_ref, old_ref, l_ref, acc_ref, s0_ref, s1_ref, o_send,
                load_sem, pair_sem, far_send, far_recv, pass_send, pass_recv,
                k_send, k_recv, v_send, v_recv, local_sem, wo_send, wo_recv, ex_send, ex_recv, out_send, out_recv):
    dp_index = lax.axis_index("dp")
    me = lax.axis_index("cp")
    tp_index = lax.axis_index("tp")
    blk = x_ref.shape[0]
    kv_heads = heads // grp
    depth = k_exp.shape[2] // kv_heads
    score_scale = head_dim ** -0.5 * math.log2(math.e)
    s_refs = (s0_ref, s1_ref)
    near = me + 1 - 2 * (me % 2)
    mid = 2 - me // 2
    end = 3 * (1 - me // 2)
    others = (near, mid, end)
    pair = tp_index + 1 - 2 * (tp_index % 2)
    far = (tp_index + 2) % 4
    far_pair = (pair + 2) % 4
    my_half = tp_index // 2
    rows = blk // pieces

    loads = [pltpu.make_async_copy(x_ref, x_all.at[tp_index], load_sem.at[0])]
    for num, (src, dst) in enumerate(((w_q_ref, w_q), (w_k_ref, w_k), (w_v_ref, w_v))):
        loads.append(pltpu.make_async_copy(src, dst, load_sem.at[num + 1]))
    for load in loads:
        load.start()

    def cp_peer(rank):
        return (dp_index, rank, tp_index)

    def tp_peer(rank):
        return (dp_index, me, rank)

    barrier = pltpu.get_barrier_semaphore()
    for rank in others:
        pl.semaphore_signal(barrier, inc=1, device_id=cp_peer(rank), device_id_type=MESH_ID)
    for shift in range(1, n_tp):
        pl.semaphore_signal(barrier, inc=1, device_id=tp_peer((tp_index + shift) % n_tp), device_id_type=MESH_ID)
    pl.semaphore_wait(barrier, n_cp - 1 + n_tp - 1)

    far_copies, pass_copies = [], []
    for num in range(pieces):
        part = pl.ds(num * rows, rows)
        far_copies.append(pltpu.make_async_remote_copy(
            src_ref=x_ref.at[part], dst_ref=x_all.at[tp_index, part], send_sem=far_send.at[num], recv_sem=far_recv.at[num],
            device_id=tp_peer(far), device_id_type=MESH_ID))
        far_copies[num].start()
        pass_copies.append(pltpu.make_async_remote_copy(
            src_ref=x_all.at[far, part], dst_ref=x_all.at[far, part], send_sem=pass_send.at[num], recv_sem=pass_recv.at[num],
            device_id=tp_peer(pair), device_id_type=MESH_ID))
    pair_copy = pltpu.make_async_remote_copy(
        src_ref=x_ref, dst_ref=x_all.at[tp_index], send_sem=pair_sem.at[0], recv_sem=pair_sem.at[1],
        device_id=tp_peer(pair), device_id_type=MESH_ID)
    pair_copy.start()

    def key_copies(step, half, rank, owner):
        k_copy = pltpu.make_async_remote_copy(
            src_ref=k_own.at[half], dst_ref=kc_all.at[owner * 2 + half], send_sem=k_send.at[step, half], recv_sem=k_recv.at[owner, half],
            device_id=cp_peer(rank), device_id_type=MESH_ID)
        at = pl.ds((owner * 2 + half) * 2, 2)
        v_copy = pltpu.make_async_remote_copy(
            src_ref=v_all.at[at], dst_ref=v_all.at[at], send_sem=v_send.at[step, half], recv_sem=v_recv.at[owner, half],
            device_id=cp_peer(rank), device_id_type=MESH_ID)
        return k_copy, v_copy

    wo_copies = [pltpu.make_async_copy(w_o_ref, w_o_all.at[0], local_sem.at[0])]
    for shift in range(1, n_tp):
        wo_copies.append(pltpu.make_async_remote_copy(
            src_ref=w_o_ref, dst_ref=w_o_all.at[shift], send_sem=wo_send.at[shift], recv_sem=wo_recv.at[shift],
            device_id=tp_peer((tp_index + shift) % n_tp), device_id_type=MESH_ID))
    ex_copies = []
    for which, (src, dst) in enumerate(((gate_ref, gate_other), (up_ref, up_other), (down_ref, down_other))):
        ex_copies.append(pltpu.make_async_remote_copy(
            src_ref=src, dst_ref=dst, send_sem=ex_send.at[which], recv_sem=ex_recv.at[which], device_id=tp_peer(pair), device_id_type=MESH_ID))

    contract = (((1,), (1,)), ((), ()))

    def project(block, start, size):
        x_blk = x_all[block, start:start + size]
        rest = lax.dot_general(w_q[...], x_blk, contract, preferred_element_type=jnp.float32).astype(jnp.bfloat16).astype(jnp.float32) * score_scale
        for term in range(3):
            part = rest.astype(jnp.bfloat16)
            for head in range(heads):
                q3_ref[block, head, term * head_dim:(term + 1) * head_dim, start:start + size] = part[head * head_dim:(head + 1) * head_dim]
            rest = rest - part.astype(jnp.float32)
        v_all[me * 4 + block, :, start:start + size] = lax.dot_general(w_v[...], x_blk, contract, preferred_element_type=jnp.float32).astype(jnp.bfloat16)
        w_kk = jnp.concatenate([w_k[...], w_k[...]], axis=0)
        k_dup[block, start:start + size, :] = lax.dot_general(x_blk, w_kk, contract, preferred_element_type=jnp.float32).astype(jnp.bfloat16)

    for block in range(n_tp):
        for head in range(heads):
            q3_ref[block, head, 3 * head_dim:, :] = jnp.zeros((depth - 3 * head_dim, blk), jnp.bfloat16)
    m_ref[...] = jnp.full(m_ref.shape, -1e30, jnp.float32)
    l_ref[...] = jnp.zeros(l_ref.shape, jnp.float32)
    acc_ref[...] = jnp.zeros(acc_ref.shape, jnp.float32)

    lane = lax.broadcasted_iota(jnp.int32, (k_own.shape[2], k_exp.shape[2]), 0)
    col = lax.broadcasted_iota(jnp.int32, (k_own.shape[2], k_exp.shape[2]), 1)
    spread = [(lane == sub * (kv_heads * head_dim) + (col // depth) * head_dim + col % head_dim).astype(jnp.bfloat16) for sub in range(2)]

    def expand(k_half, at):
        for sub in range(2):
            k_exp[at * 2 + sub] = jnp.dot(k_half, spread[sub], preferred_element_type=jnp.float32).astype(jnp.bfloat16)

    def score(head, block, at, masked):
        kv = head // grp
        scores = jnp.dot(k_exp[at, :, kv * depth:(kv + 1) * depth], q3_ref[block, head], preferred_element_type=jnp.float32)
        if masked:
            k_pos = lax.broadcasted_iota(jnp.int32, (blk, blk), 0)
            q_pos = lax.broadcasted_iota(jnp.int32, (blk, blk), 1)
            scores = jnp.where(k_pos <= q_pos, scores, -1e30)
        s_refs[head % 2][...] = scores
        old = m_ref[block, head]
        old_ref[head] = old
        m_ref[block, head] = jnp.maximum(old, jnp.max(scores, axis=0, keepdims=True))

    def mix(head, block, at):
        kv = head // grp
        top = m_ref[block, head]
        prob = jnp.exp2(s_refs[head % 2][...] - top)
        part = jnp.sum(prob.reshape(blk // 8, 8, blk), axis=0)
        mixed = jnp.dot(v_all[at, kv * head_dim:(kv + 1) * head_dim, :], prob.astype(jnp.bfloat16), preferred_element_type=jnp.float32)
        rescale = jnp.exp2(old_ref[head] - top)
        l_ref[block, head] = l_ref[block, head] * rescale + part
        acc_ref[block, head] = acc_ref[block, head] * rescale + mixed

    def run(count, place, masked):
        block, at = place(0)
        score(0, block, at, masked)

        def body(num, carry):
            block, at = place(num)
            next_block, next_at = place(num + 1 - (num + 1) // count)
            for head in range(heads):
                if head + 1 < heads:
                    score(head + 1, block, at, masked)
                else:
                    score(0, next_block, next_at, masked)
                mix(head, block, at)
            return carry

        lax.fori_loop(0, count, body, 0)

    low = lax.broadcasted_iota(jnp.int32, k_dup.shape[1:], 1) < k_dup.shape[2] // 2

    def finish_half(half):
        k_own[half] = jnp.where(low, k_dup[2 * half].astype(jnp.float32), k_dup[2 * half + 1].astype(jnp.float32)).astype(jnp.bfloat16)
        expand(k_own[half], me * 2 + half)
        for step, rank in enumerate(others):
            @pl.when((1 - half) + (me - rank + 3) // 4 > 0)
            def _():
                for copy in key_copies(step, half, rank, me):
                    copy.start()

    def send_out(block):
        shift = (block - tp_index + n_tp) % n_tp
        for head in range(heads):
            total = jnp.sum(l_ref[block, head], axis=0, keepdims=True)
            o_send[block, head * head_dim:(head + 1) * head_dim, :] = (acc_ref[block, head] / total).astype(jnp.bfloat16)

        @pl.when(shift == 0)
        def _():
            out_copy(shift, block).start()

        @pl.when(shift > 0)
        def _():
            far_out(shift, block).start()

    def out_copy(shift, block):
        return pltpu.make_async_copy(o_send.at[block], o_ref.at[shift], local_sem.at[1])

    def far_out(shift, block):
        return pltpu.make_async_remote_copy(
            src_ref=o_send.at[block], dst_ref=o_ref.at[shift], send_sem=out_send.at[shift], recv_sem=out_recv.at[shift],
            device_id=tp_peer(block), device_id_type=MESH_ID)

    for load in loads:
        load.wait()
    project(tp_index, 0, blk)
    pair_copy.wait_recv()
    project(pair, 0, blk)
    finish_half(my_half)
    run(2, lambda num: (2 * my_half + num, me * 4 + 2 * my_half + num), True)
    for num in range(pieces):
        far_copies[num].wait_recv()
        pass_copies[num].start()
        project(far, num * rows, rows)
        pass_copies[num].wait_recv()
        project(far_pair, num * rows, rows)
    far_half = 1 - my_half
    finish_half(far_half)
    for copy in wo_copies + ex_copies:
        copy.start()
    run(2, lambda num: (2 * far_half + num, me * 4 + 2 * far_half + num), True)

    def place_local(num):
        late = (num + 2) // 4
        block = (1 - late) * (1 + 2 * num) + late * (1 + num // 2)
        half = (1 - late) * num
        return block, me * 4 + half * 2 + late * (num % 2)

    run(6, place_local, False)

    def visit_rank(turn, carry):
        step, part = turn // 2, turn % 2
        rank = ((2 - step) // 2) * near + (step % 2) * mid + (step // 2) * end
        below = (me - rank + 3) // 4

        @pl.when(part == 0)
        def _():
            for copy in key_copies(0, 0, rank, rank):
                copy.wait_recv()
            expand(kc_all[rank * 2], rank * 2)

            @pl.when(rank > me)
            def _():
                for copy in key_copies(0, 1, rank, rank):
                    copy.wait_recv()
                expand(kc_all[rank * 2 + 1], rank * 2 + 1)

        def place(num):
            two = part * 2 + num // 2
            block = below * (two - 1 + 3 * (1 - (two + 3) // 4) + two // 3) + (1 - below) * (2 + part)
            half = (1 - below) * (two % 2)
            return block, rank * 4 + half * 2 + num % 2

        run(4, place, False)

        @pl.when(turn == 2 * (n_cp - 1) - 2)
        def _():
            send_out(2)
            send_out(0)

        return carry

    lax.fori_loop(0, 2 * (n_cp - 1), visit_rank, 0)
    send_out(3)
    send_out(1)

    pair_copy.wait_send()
    for num in range(pieces):
        far_copies[num].wait_send()
        pass_copies[num].wait_send()
    for step, rank in enumerate(others):
        for copy in key_copies(step, 0, rank, me):
            copy.wait_send()

        @pl.when(rank < me)
        def _():
            for copy in key_copies(step, 1, rank, me):
                copy.wait_send()

    out_copy(0, tp_index).wait()
    for shift in range(1, n_tp):
        far_out(shift, (tp_index + shift) % n_tp).wait()
    for copy in wo_copies + ex_copies:
        copy.wait()


def attention(x_loc, w_q, w_k, w_v, w_o, experts, n_cp, n_tp, head_dim):
    blk, hid = x_loc.shape
    q_depth = w_q.shape[0]
    kv_depth = w_k.shape[0]
    heads = q_depth // head_dim
    kv_heads = kv_depth // head_dim
    grp = heads // kv_heads
    depth = 128
    pieces = 4
    pairs = heads * (n_tp * blk) ** 2 * n_cp // 2
    any_spec = pl.BlockSpec(memory_space=pl.ANY)
    dma = pltpu.SemaphoreType.DMA
    return pl.pallas_call(
        functools.partial(attn_kernel, n_cp, n_tp, heads, grp, head_dim, pieces),
        out_shape=(
            jax.ShapeDtypeStruct((n_tp, q_depth, blk), jnp.bfloat16),
            jax.ShapeDtypeStruct((n_tp, q_depth, hid), jnp.bfloat16),
        ) + tuple(jax.ShapeDtypeStruct(one.shape, one.dtype) for one in experts),
        in_specs=[any_spec] * 8,
        out_specs=(any_spec,) * 5,
        scratch_shapes=[
            pltpu.VMEM((n_tp, blk, hid), jnp.bfloat16),
            pltpu.VMEM((q_depth, hid), jnp.bfloat16),
            pltpu.VMEM((kv_depth, hid), jnp.bfloat16),
            pltpu.VMEM((kv_depth, hid), jnp.bfloat16),
            pltpu.VMEM((n_tp, blk, 2 * kv_depth), jnp.bfloat16),
            pltpu.VMEM((2, blk, 2 * kv_depth), jnp.bfloat16),
            pltpu.VMEM((n_tp, heads, depth, blk), jnp.bfloat16),
            pltpu.VMEM((2 * n_cp, blk, 2 * kv_depth), jnp.bfloat16),
            pltpu.VMEM((4 * n_cp, kv_depth, blk), jnp.bfloat16),
            pltpu.VMEM((4 * n_cp, blk, kv_heads * depth), jnp.bfloat16),
            pltpu.VMEM((n_tp, heads, 1, blk), jnp.float32),
            pltpu.VMEM((heads, 1, blk), jnp.float32),
            pltpu.VMEM((n_tp, heads, 8, blk), jnp.float32),
            pltpu.VMEM((n_tp, heads, head_dim, blk), jnp.float32),
            pltpu.VMEM((blk, blk), jnp.float32),
            pltpu.VMEM((blk, blk), jnp.float32),
            pltpu.VMEM((n_tp, q_depth, blk), jnp.bfloat16),
            dma((4,)), dma((2,)), dma((pieces,)), dma((pieces,)), dma((pieces,)), dma((pieces,)),
            dma((n_cp - 1, 2)), dma((n_cp, 2)), dma((n_cp - 1, 2)), dma((n_cp, 2)), dma((2,)),
            dma((n_tp,)), dma((n_tp,)), dma((3,)), dma((3,)), dma((n_tp,)), dma((n_tp,)),
        ],
        compiler_params=pltpu.CompilerParams(collective_id=2, has_side_effects=True, vmem_limit_bytes=67043328),
        cost_estimate=pl.CostEstimate(flops=4 * pairs * 64, bytes_accessed=40 * 1024 * 1024, transcendentals=pairs),
        name="causal_attention",
    )(x_loc, w_q, w_k, w_v, w_o, *experts)


def flip_bits(index, pattern, n_bits):
    result = 0
    for bit in range(n_bits):
        digit = (index // (1 << bit)) % 2
        result = result + ((1 - digit) if (pattern >> bit) & 1 else digit) * (1 << bit)
    return result


def expert_kernel(n_chips, order, rounds, h_ref, slot_row, slot_col, gates_ref, gate_a, gate_b, up_a, up_b, down_a, down_b, y_ref,
                  send_buf, recv, w_gate, w_up, w_down, act, z_out, z_in, y_acc, y_out, load_sem, own_sem, send_sem, recv_sem, back_sem, home_sem):
    n_bits = n_chips.bit_length() - 1
    dp_index = lax.axis_index("dp")
    cp_index = lax.axis_index("cp")
    tp_index = lax.axis_index("tp")
    core = tp_index % 2
    chip = cp_index * 2 + tp_index // 2

    def peer(pattern):
        other = flip_bits(chip, pattern, n_bits)
        return (dp_index, other // 2, (other % 2) * 2 + core)

    loads = []
    for half, refs in enumerate(((gate_a, up_a, down_a), (gate_b, up_b, down_b))):
        for which, (src, dst) in enumerate(zip(refs, (w_gate, w_up, w_down))):
            loads.append(pltpu.make_async_copy(src.at[0], dst.at[half], load_sem.at[half, which]))
    for load in loads:
        load.start()
    barrier = pltpu.get_barrier_semaphore()
    for pattern in range(1, n_chips):
        pl.semaphore_signal(barrier, inc=1, device_id=peer(pattern), device_id_type=MESH_ID)
    pl.semaphore_wait(barrier, n_chips - 1)

    rows = recv.shape[1]
    hid = recv.shape[2]
    tok = h_ref.shape[0]
    ffn = w_gate.shape[2]
    tile = 256

    def pick(pattern):
        slots = lax.broadcasted_iota(jnp.int32, (rows, tok), 0) + pattern * rows
        chosen = (slots == slot_row[0:1, :]) | (slots == slot_row[1:2, :])
        return jnp.dot(chosen.astype(jnp.bfloat16), h_ref[...], preferred_element_type=jnp.float32).astype(jnp.bfloat16)

    sends = {}
    for pattern in order:
        sends[pattern] = pltpu.make_async_remote_copy(
            src_ref=send_buf.at[pattern], dst_ref=recv.at[pattern], send_sem=send_sem.at[pattern], recv_sem=recv_sem.at[pattern],
            device_id=peer(pattern), device_id_type=MESH_ID)
    late = None
    for pattern in order:
        send_buf[pattern] = pick(pattern)
        if late is not None:
            sends[late].start()
        late = pattern
    recv[0] = pick(0)
    sends[late].start()
    y_acc[...] = h_ref[...].astype(jnp.float32)

    def combine(pattern):
        slots = lax.broadcasted_iota(jnp.int32, (tok, rows), 1) + pattern * rows
        z_blk = z_in[pattern]
        for choice in range(slot_row.shape[0]):
            chosen = (slots == slot_col[:, choice:choice + 1]).astype(jnp.bfloat16)
            y_acc[...] = y_acc[...] + gates_ref[:, choice:choice + 1] * jnp.dot(chosen, z_blk, preferred_element_type=jnp.float32)

    backs = {}
    for turn, (first, second) in enumerate(rounds):
        for pattern in (first, second):
            if pattern:
                sends[pattern].wait_recv()
        for half in range(2):
            if turn == 0:
                loads[half * 3].wait()
                loads[half * 3 + 1].wait()

        x_blk = jnp.concatenate([recv[first], recv[second]], axis=0)

        def half_step(half, carry):
            for col in range(0, ffn, tile):
                gate_pre = jnp.dot(x_blk, w_gate[half, :, col:col + tile], preferred_element_type=jnp.float32)
                up_pre = jnp.dot(x_blk, w_up[half, :, col:col + tile], preferred_element_type=jnp.float32)
                act[half, :, col:col + tile] = (jax.nn.silu(gate_pre) * up_pre).astype(jnp.bfloat16)
            return carry

        lax.fori_loop(0, 2, half_step, 0)
        if turn == 0:
            for half in range(2):
                loads[half * 3 + 2].wait()

        def out_step(col, carry):
            at = pl.multiple_of(col * tile, tile)
            z_blk = jnp.dot(act[0], w_down[0, :, pl.ds(at, tile)], preferred_element_type=jnp.float32)
            z_blk = z_blk + jnp.dot(act[1], w_down[1, :, pl.ds(at, tile)], preferred_element_type=jnp.float32)
            z_blk = z_blk.astype(jnp.bfloat16)
            z_out[first, :, pl.ds(at, tile)] = z_blk[:rows]
            z_out[second, :, pl.ds(at, tile)] = z_blk[rows:]
            return carry

        lax.fori_loop(0, hid // tile, out_step, 0)
        for pattern in (first, second):
            if pattern:
                backs[pattern] = pltpu.make_async_remote_copy(
                    src_ref=z_out.at[pattern], dst_ref=z_in.at[pattern], send_sem=back_sem.at[pattern], recv_sem=home_sem.at[pattern],
                    device_id=peer(pattern), device_id_type=MESH_ID)
                backs[pattern].start()
    z_in[0] = z_out[0]
    combine(0)
    for pattern in order:
        backs[pattern].wait_recv()
        combine(pattern)
    y_out[...] = y_acc[...].astype(jnp.bfloat16)
    result = pltpu.make_async_copy(y_out, y_ref, own_sem.at[0])
    result.start()
    for pattern in order:
        sends[pattern].wait_send()
        backs[pattern].wait_send()
    result.wait()


def expert_layer(h_loc, slot_idx, gates, n_chips, own_weights, other_weights):
    tok, hid = h_loc.shape
    rows = slot_idx.shape[1] * tok // n_chips
    ffn = own_weights[0].shape[2]
    order = (1, 4, 6, 5, 7, 2, 3)
    rounds = ((0, 1), (4, 6), (5, 7), (2, 3))
    weights = []
    for own, other in zip(own_weights, other_weights):
        weights += [own, other]
    any_spec = pl.BlockSpec(memory_space=pl.ANY)
    vmem = pl.BlockSpec(memory_space=pltpu.VMEM)
    flops = 2 * 3 * n_chips * rows * hid * 2 * ffn
    return pl.pallas_call(
        functools.partial(expert_kernel, n_chips, order, rounds),
        out_shape=jax.ShapeDtypeStruct((tok, hid), jnp.bfloat16),
        in_specs=[vmem] * 4 + [any_spec] * 6,
        out_specs=any_spec,
        scratch_shapes=[
            pltpu.VMEM((n_chips, rows, hid), jnp.bfloat16),
            pltpu.VMEM((n_chips, rows, hid), jnp.bfloat16),
            pltpu.VMEM((2, hid, ffn), jnp.bfloat16),
            pltpu.VMEM((2, hid, ffn), jnp.bfloat16),
            pltpu.VMEM((2, ffn, hid), jnp.bfloat16),
            pltpu.VMEM((2, 2 * rows, ffn), jnp.bfloat16),
            pltpu.VMEM((n_chips, rows, hid), jnp.bfloat16),
            pltpu.VMEM((n_chips, rows, hid), jnp.bfloat16),
            pltpu.VMEM((tok, hid), jnp.float32),
            pltpu.VMEM((tok, hid), jnp.bfloat16),
            pltpu.SemaphoreType.DMA((2, 3)),
            pltpu.SemaphoreType.DMA((1,)),
            pltpu.SemaphoreType.DMA((n_chips,)),
            pltpu.SemaphoreType.DMA((n_chips,)),
            pltpu.SemaphoreType.DMA((n_chips,)),
            pltpu.SemaphoreType.DMA((n_chips,)),
        ],
        compiler_params=pltpu.CompilerParams(collective_id=1, has_side_effects=True, vmem_limit_bytes=58 * 1024 * 1024),
        cost_estimate=pl.CostEstimate(flops=flops, bytes_accessed=32 * 1024 * 1024, transcendentals=n_chips * rows * 2 * ffn),
        name="expert_layer",
    )(h_loc, slot_idx.T, slot_idx, gates, *weights)


def solution(mesh):
    n_cp = mesh.shape["cp"]
    n_tp = mesh.shape["tp"]
    row_spec = P(("dp", "cp", "tp"), None)
    head_spec = P(None, "tp", None)
    expert_spec = P(("cp", "tp"), None, None)

    def device_step(x_loc, w_q, w_k, w_v, w_o, ids_loc, gates_loc, w_gate, w_up, w_down):
        tok_dev, hid_dim = x_loc.shape
        top_k = ids_loc.shape[1]
        heads = w_q.shape[1]
        head_dim = w_q.shape[2]
        local_exp = w_gate.shape[0]
        n_experts = local_exp * n_cp * n_tp // 2
        capacity = top_k * tok_dev // n_experts
        chip = lax.axis_index("cp") * 2 + lax.axis_index("tp") // 2

        choice_hot = (ids_loc[:, :, None] == jnp.arange(n_experts)[None, None, :])
        token_hot = jnp.sum(choice_hot.astype(jnp.bfloat16), axis=1)
        earlier = (lax.broadcasted_iota(jnp.int32, (tok_dev, tok_dev), 0) > lax.broadcasted_iota(jnp.int32, (tok_dev, tok_dev), 1)).astype(jnp.bfloat16)
        rank_in = jnp.dot(earlier, token_hot, preferred_element_type=jnp.float32).astype(jnp.int32)
        place = rank_in + (jnp.arange(n_experts, dtype=jnp.int32) ^ chip)[None, :] * capacity
        dest_idx = jnp.sum(jnp.where(choice_hot, place[:, None, :], 0), axis=2)

        w_qkv_t = [one.transpose(1, 2, 0).reshape(-1, hid_dim) for one in (w_q, w_k, w_v)]
        out_t, w_o_all, *other_weights = attention(x_loc, *w_qkv_t, w_o.reshape(heads * head_dim, hid_dim), (w_gate, w_up, w_down), n_cp, n_tp, head_dim)
        out_t = out_t.reshape(n_tp * heads * head_dim, tok_dev)
        w_o_all = w_o_all.reshape(n_tp * heads * head_dim, hid_dim)
        attn_rows = lax.dot_general(out_t, w_o_all, (((0,), (0,)), ((), ())), preferred_element_type=jnp.float32)
        h_loc = (x_loc.astype(jnp.float32) + attn_rows).astype(jnp.bfloat16)

        return expert_layer(h_loc, dest_idx, gates_loc, n_experts, (w_gate, w_up, w_down), other_weights)

    return jax.shard_map(device_step, mesh=mesh, in_specs=(row_spec, head_spec, head_spec, head_spec, P("tp", None, None), row_spec, row_spec, expert_spec, expert_spec, expert_spec), out_specs=row_spec, check_vma=False)
```

time: 243 us -> 227 us (0.934)
  Pallas kernels: 227 us -> 218 us
  matrix products: 9.52 us -> 4.64 us
    pallas_call x1 -> x0, Pallas kernels: 28.5 us -> none  [project_rows(): pl.pallas_call(functools.partial(project_kernel, pieces), out_shape=(jax....]
    pallas_call x1, Pallas kernels: 103 us -> 118 us  [attention(): pl.pallas_call(functools.partial(attn_kernel, n_cp, n_tp, heads, grp, hea...]
    dot_general x3 -> x0, matrix products: 8.03 us -> none  [the longest x2 5.41 us: device_step(): jnp.dot(take, z_full, preferred_element_type=jnp.float32)]
    pallas_call x1, Pallas kernels: 96 us -> 100 us  [expert_layer(): pl.pallas_call(functools.partial(expert_kernel, n_chips, order, rounds),...]
    dot_general x1, matrix products: 1.27 us -> 4.42 us  [device_step(): lax.dot_general(out_t, w_o_all, (((0,), (0,)), ((), ())), preferred_eleme...]
where the time goes in v4:
time: 227 us
  Pallas kernels  218 us (96%)
  matrix products  4.64 us (2%)
  local copies, waits for them, and re-layouts  4.01 us (2%)
    pallas_call x1, Pallas kernels, attention(): pl.pallas_call(functools.partial(attn_kernel, n_cp, n_tp, heads, grp, hea...  118 us
    pallas_call x1, Pallas kernels, expert_layer(): pl.pallas_call(functools.partial(expert_kernel, n_chips, order, rounds),...  100 us

profile of v4, /device:TPU:0, one launch (start us, length us, event | category | flops | bytes accessed | tf_op | source)
XLA Modules:
  0.0 227.0 jit_solution(2657554128825996754)
XLA Ops:
  0.0 118.0 %causal_attention.1 = (bf16[4,256,512]{2,1,0:T(8,128)(2,1)}, bf16[4,256,1024]{2,1,0:T(8,128)(2,1)}, bf16[1,1024,1792]{2,1,0:T(8,128)(2,1)}, bf16[1,1024,1792]{2,1,0:T(8,128)(2,1)}, bf16[1,1792,1024]{2,1,0:T(8,128)(2,1)}) custom-call(bf16[512,1024]{1,0:T(8,128)(2,1)} %x_ref.1, bf16[256,1024]{1,0:T(8,128)(2,1)} %bitcast.19, bf16[64,1024]{1,0:T(8,128)(2,1)} %bitcast.21, ...), custom_call_target="tpu_custom_call" | custom-call | flops 17179869184 | bytes 41943040 | tf_op jit(solution)/shard_map/causal_attention/pallas_call | solution.py:288
  118.0 0.0 copy-start.1
  118.0 0.0 copy-start.2
  118.0 4.4 %fusion.h_ref = bf16[512,1024]{1,0:T(8,128)(2,1)} fusion(bf16[512,1024]{1,0:T(8,128)(2,1)} %x_ref.1, bf16[4,256,512]{2,1,0:T(8,128)(2,1)} %get-tuple-element.10, bf16[4,256,1024]{2,1,0:T(8,128)(2,1)} %get-tuple-element.11), kind=kOutput, calls=%fused_computation.1 | convolution fusion | flops 1075314688 | bytes 5242880 | tf_op jit(solution)/shard_map/dot_general | solution.py:512
  122.4 0.0 copy-done.1
  122.5 0.2 fusion.1
  122.7 0.1 select_reduce_fusion
  122.8 0.0 copy-start
  122.8 0.9 copy.17.slot_col
  123.6 0.0 copy-done.2
  123.6 0.9 copy.18.gates_ref
  124.5 0.0 copy-done
  124.5 100.2 %expert_layer.1 = bf16[512,1024]{1,0:T(8,128)(2,1)} custom-call(bf16[512,1024]{1,0:T(8,128)(2,1)} %fusion.h_ref, s32[2,512]{1,0:T(2,128)} %bitcast.18, s32[512,2]{1,0:T(8,128)} %copy.17.slot_col, f32[512,2]{1,0:T(8,128)} %copy.18.gates_ref, bf16[1,1024,1792]{2,1,0:T(8,128)(2,1)} %gate_a.1, bf16[1,1024,1792]{2,1,0:T(8,128)(2,1)} %get-tuple-element.12.gate_b, ...), custom_call_target="tpu_custom_call" | custom-call | flops 22548578304 | bytes 33554432 | tf_op jit(solution)/shard_map/expert_layer/pallas_call | solution.py:455
  224.8 2.3 copy.21
  (2 shorter events, 0.0 us)
Async XLA Ops:
  118.0 4.4 %copy-start.1 = (s32[512,2]{0,1:T(2,128)S(1)}, s32[512,2]{0,1:T(2,128)}, u32[]{:S(2)}) copy-start(s32[512,2]{0,1:T(2,128)} %param.15) | copy-start | bytes 12292
  118.0 5.6 %copy-start.2 = (f32[512,2]{0,1:T(2,128)S(1)}, f32[512,2]{0,1:T(2,128)}, u32[]{:S(2)}) copy-start(f32[512,2]{0,1:T(2,128)} %param.16) | copy-start | bytes 12292
  122.8 1.7 copy-start

commit v5 on v4

--- a/solution.py
+++ b/solution.py
@@ -13,8 +13,8 @@
 
 
 def attn_kernel(n_cp, n_tp, heads, grp, head_dim, pieces, x_ref, w_q_ref, w_k_ref, w_v_ref, w_o_ref, gate_ref, up_ref, down_ref,
-                o_ref, w_o_all, gate_other, up_other, down_other,
-                x_all, w_q, w_k, w_v, k_dup, k_own, q3_ref, kc_all, v_all, k_exp, m_ref, old_ref, l_ref, acc_ref, s0_ref, s1_ref, o_send,
+                h_ref, gate_other, up_other, down_other,
+                x_all, w_q, w_k, w_v, k_dup, k_own, q3_ref, kc_all, v_all, k_exp, m_ref, old_ref, top_ref, l_ref, acc_ref, s0_ref, s1_ref, o_send, o_all, w_o_all, h_acc, h_out,
                 load_sem, pair_sem, far_send, far_recv, pass_send, pass_recv,
                 k_send, k_recv, v_send, v_recv, local_sem, wo_send, wo_recv, ex_send, ex_recv, out_send, out_recv):
     dp_index = lax.axis_index("dp")
@@ -128,11 +128,13 @@
         s_refs[head % 2][...] = scores
         old = m_ref[block, head]
         old_ref[head] = old
-        m_ref[block, head] = jnp.maximum(old, jnp.max(scores, axis=0, keepdims=True))
+        top = jnp.maximum(old, jnp.max(scores, axis=0, keepdims=True))
+        top_ref[head] = top
+        m_ref[block, head] = top
 
     def mix(head, block, at):
         kv = head // grp
-        top = m_ref[block, head]
+        top = top_ref[head]
         prob = jnp.exp2(s_refs[head % 2][...] - top)
         part = jnp.sum(prob.reshape(blk // 8, 8, blk), axis=0)
         mixed = jnp.dot(v_all[at, kv * head_dim:(kv + 1) * head_dim, :], prob.astype(jnp.bfloat16), preferred_element_type=jnp.float32)
@@ -174,20 +176,13 @@
             total = jnp.sum(l_ref[block, head], axis=0, keepdims=True)
             o_send[block, head * head_dim:(head + 1) * head_dim, :] = (acc_ref[block, head] / total).astype(jnp.bfloat16)
 
-        @pl.when(shift == 0)
-        def _():
-            out_copy(shift, block).start()
-
         @pl.when(shift > 0)
         def _():
             far_out(shift, block).start()
 
-    def out_copy(shift, block):
-        return pltpu.make_async_copy(o_send.at[block], o_ref.at[shift], local_sem.at[1])
-
     def far_out(shift, block):
         return pltpu.make_async_remote_copy(
-            src_ref=o_send.at[block], dst_ref=o_ref.at[shift], send_sem=out_send.at[shift], recv_sem=out_recv.at[shift],
+            src_ref=o_send.at[block], dst_ref=o_all.at[shift], send_sem=out_send.at[shift], recv_sem=out_recv.at[shift],
             device_id=tp_peer(block), device_id_type=MESH_ID)
 
     for load in loads:
@@ -266,11 +261,22 @@
             for copy in key_copies(step, 1, rank, me):
                 copy.wait_send()
 
-    out_copy(0, tp_index).wait()
-    for shift in range(1, n_tp):
-        far_out(shift, (tp_index + shift) % n_tp).wait()
-    for copy in wo_copies + ex_copies:
+    wo_copies[0].wait()
+    for shift in (0, 1, 3, 2):
+        if shift:
+            far_out(shift, (tp_index + shift) % n_tp).wait()
+            wo_copies[shift].wait()
+            o_blk = o_all[shift]
+        else:
+            o_blk = o_send[tp_index]
+        h_part = lax.dot_general(o_blk, w_o_all[shift], (((0,), (0,)), ((), ())), preferred_element_type=jnp.float32)
+        h_acc[...] = h_acc[...] + h_part if shift else h_part
+    h_out[...] = (x_all[tp_index].astype(jnp.float32) + h_acc[...]).astype(jnp.bfloat16)
+    result = pltpu.make_async_copy(h_out, h_ref, local_sem.at[1])
+    result.start()
+    for copy in ex_copies:
         copy.wait()
+    result.wait()
 
 
 def attention(x_loc, w_q, w_k, w_v, w_o, experts, n_cp, n_tp, head_dim):
@@ -288,11 +294,10 @@
     return pl.pallas_call(
         functools.partial(attn_kernel, n_cp, n_tp, heads, grp, head_dim, pieces),
         out_shape=(
-            jax.ShapeDtypeStruct((n_tp, q_depth, blk), jnp.bfloat16),
-            jax.ShapeDtypeStruct((n_tp, q_depth, hid), jnp.bfloat16),
+            jax.ShapeDtypeStruct((blk, hid), jnp.bfloat16),
         ) + tuple(jax.ShapeDtypeStruct(one.shape, one.dtype) for one in experts),
         in_specs=[any_spec] * 8,
-        out_specs=(any_spec,) * 5,
+        out_specs=(any_spec,) * 4,
         scratch_shapes=[
             pltpu.VMEM((n_tp, blk, hid), jnp.bfloat16),
             pltpu.VMEM((q_depth, hid), jnp.bfloat16),
@@ -306,11 +311,16 @@
             pltpu.VMEM((4 * n_cp, blk, kv_heads * depth), jnp.bfloat16),
             pltpu.VMEM((n_tp, heads, 1, blk), jnp.float32),
             pltpu.VMEM((heads, 1, blk), jnp.float32),
+            pltpu.VMEM((heads, 1, blk), jnp.float32),
             pltpu.VMEM((n_tp, heads, 8, blk), jnp.float32),
             pltpu.VMEM((n_tp, heads, head_dim, blk), jnp.float32),
             pltpu.VMEM((blk, blk), jnp.float32),
             pltpu.VMEM((blk, blk), jnp.float32),
             pltpu.VMEM((n_tp, q_depth, blk), jnp.bfloat16),
+            pltpu.VMEM((n_tp, q_depth, blk), jnp.bfloat16),
+            pltpu.VMEM((n_tp, q_depth, hid), jnp.bfloat16),
+            pltpu.VMEM((blk, hid), jnp.float32),
+            pltpu.VMEM((blk, hid), jnp.bfloat16),
             dma((4,)), dma((2,)), dma((pieces,)), dma((pieces,)), dma((pieces,)), dma((pieces,)),
             dma((n_cp - 1, 2)), dma((n_cp, 2)), dma((n_cp - 1, 2)), dma((n_cp, 2)), dma((2,)),
             dma((n_tp,)), dma((n_tp,)), dma((3,)), dma((3,)), dma((n_tp,)), dma((n_tp,)),
@@ -329,8 +339,8 @@
     return result
 
 
-def expert_kernel(n_chips, order, rounds, h_ref, slot_row, slot_col, gates_ref, gate_a, gate_b, up_a, up_b, down_a, down_b, y_ref,
-                  send_buf, recv, w_gate, w_up, w_down, act, z_out, z_in, y_acc, y_out, load_sem, own_sem, send_sem, recv_sem, back_sem, home_sem):
+def expert_kernel(n_chips, order, rounds, h_ref, slot_row, gate_row, gate_a, gate_b, up_a, up_b, down_a, down_b, y_ref,
+                  send_buf, recv, w_gate, w_up, w_down, act, z_out, z_in, y_acc, load_sem, own_sem, send_sem, recv_sem, back_sem, home_sem):
     n_bits = n_chips.bit_length() - 1
     dp_index = lax.axis_index("dp")
     cp_index = lax.axis_index("cp")
@@ -378,13 +388,14 @@
     recv[0] = pick(0)
     sends[late].start()
     y_acc[...] = h_ref[...].astype(jnp.float32)
+    by_token = jnp.concatenate([slot_row[...].astype(jnp.float32), gate_row[...], jnp.zeros((8 - 2 * slot_row.shape[0], tok), jnp.float32)], axis=0).T
 
     def combine(pattern):
-        slots = lax.broadcasted_iota(jnp.int32, (tok, rows), 1) + pattern * rows
+        slots = (lax.broadcasted_iota(jnp.int32, (tok, rows), 1) + pattern * rows).astype(jnp.float32)
         z_blk = z_in[pattern]
         for choice in range(slot_row.shape[0]):
-            chosen = (slots == slot_col[:, choice:choice + 1]).astype(jnp.bfloat16)
-            y_acc[...] = y_acc[...] + gates_ref[:, choice:choice + 1] * jnp.dot(chosen, z_blk, preferred_element_type=jnp.float32)
+            chosen = (slots == by_token[:, choice:choice + 1]).astype(jnp.bfloat16)
+            y_acc[...] = y_acc[...] + by_token[:, slot_row.shape[0] + choice:slot_row.shape[0] + choice + 1] * jnp.dot(chosen, z_blk, preferred_element_type=jnp.float32)
 
     backs = {}
     for turn, (first, second) in enumerate(rounds):
@@ -431,8 +442,7 @@
     for pattern in order:
         backs[pattern].wait_recv()
         combine(pattern)
-    y_out[...] = y_acc[...].astype(jnp.bfloat16)
-    result = pltpu.make_async_copy(y_out, y_ref, own_sem.at[0])
+    result = pltpu.make_async_copy(y_acc, y_ref, own_sem.at[0])
     result.start()
     for pattern in order:
         sends[pattern].wait_send()
@@ -454,8 +464,8 @@
     flops = 2 * 3 * n_chips * rows * hid * 2 * ffn
     return pl.pallas_call(
         functools.partial(expert_kernel, n_chips, order, rounds),
-        out_shape=jax.ShapeDtypeStruct((tok, hid), jnp.bfloat16),
-        in_specs=[vmem] * 4 + [any_spec] * 6,
+        out_shape=jax.ShapeDtypeStruct((tok, hid), jnp.float32),
+        in_specs=[vmem] * 3 + [any_spec] * 6,
         out_specs=any_spec,
         scratch_shapes=[
             pltpu.VMEM((n_chips, rows, hid), jnp.bfloat16),
@@ -467,7 +477,6 @@
             pltpu.VMEM((n_chips, rows, hid), jnp.bfloat16),
             pltpu.VMEM((n_chips, rows, hid), jnp.bfloat16),
             pltpu.VMEM((tok, hid), jnp.float32),
-            pltpu.VMEM((tok, hid), jnp.bfloat16),
             pltpu.SemaphoreType.DMA((2, 3)),
             pltpu.SemaphoreType.DMA((1,)),
             pltpu.SemaphoreType.DMA((n_chips,)),
@@ -478,7 +487,7 @@
         compiler_params=pltpu.CompilerParams(collective_id=1, has_side_effects=True, vmem_limit_bytes=58 * 1024 * 1024),
         cost_estimate=pl.CostEstimate(flops=flops, bytes_accessed=32 * 1024 * 1024, transcendentals=n_chips * rows * 2 * ffn),
         name="expert_layer",
-    )(h_loc, slot_idx.T, slot_idx, gates, *weights)
+    )(h_loc, slot_idx.T, gates.T, *weights)
 
 
 def solution(mesh):
@@ -506,12 +515,7 @@
         dest_idx = jnp.sum(jnp.where(choice_hot, place[:, None, :], 0), axis=2)
 
         w_qkv_t = [one.transpose(1, 2, 0).reshape(-1, hid_dim) for one in (w_q, w_k, w_v)]
-        out_t, w_o_all, *other_weights = attention(x_loc, *w_qkv_t, w_o.reshape(heads * head_dim, hid_dim), (w_gate, w_up, w_down), n_cp, n_tp, head_dim)
-        out_t = out_t.reshape(n_tp * heads * head_dim, tok_dev)
-        w_o_all = w_o_all.reshape(n_tp * heads * head_dim, hid_dim)
-        attn_rows = lax.dot_general(out_t, w_o_all, (((0,), (0,)), ((), ())), preferred_element_type=jnp.float32)
-        h_loc = (x_loc.astype(jnp.float32) + attn_rows).astype(jnp.bfloat16)
-
-        return expert_layer(h_loc, dest_idx, gates_loc, n_experts, (w_gate, w_up, w_down), other_weights)
+        h_loc, *other_weights = attention(x_loc, *w_qkv_t, w_o.reshape(heads * head_dim, hid_dim), (w_gate, w_up, w_down), n_cp, n_tp, head_dim)
+        return expert_layer(h_loc, dest_idx, gates_loc, n_experts, (w_gate, w_up, w_down), other_weights).astype(jnp.bfloat16)
 
     return jax.shard_map(device_step, mesh=mesh, in_specs=(row_spec, head_spec, head_spec, head_spec, P("tp", None, None), row_spec, row_spec, expert_spec, expert_spec, expert_spec), out_specs=row_spec, check_vma=False)

time: 227 us -> 220 us (0.969)
  other arithmetic: 0.06 us -> 4.75 us
  matrix products: 4.64 us -> 0.22 us
  local copies, waits for them, and re-layouts: 4.01 us -> 0 us
  Pallas kernels: 218 us -> 215 us
    dot_general x1 -> x0, matrix products: 4.42 us -> none  [device_step(): lax.dot_general(out_t, w_o_all, (((0,), (0,)), ((), ())), preferred_eleme...]
    pallas_call x1, Pallas kernels: 118 us -> 115 us  [attention(): pl.pallas_call(functools.partial(attn_kernel, n_cp, n_tp, heads, grp, hea...]
    unnamed x8 -> x0, local copies, waits for them, and re-layouts: 3.15 us -> none
    convert_element_type x0 -> x1, other arithmetic: none -> 2.73 us  [device_step(): expert_layer(h_loc, dest_idx, gates_loc, n_experts, (w_gate, w_up, w_down...]
where the time goes in v5:
time: 220 us
  Pallas kernels  215 us (98%)
  other arithmetic  4.75 us (2%)
    pallas_call x1, Pallas kernels, attention(): pl.pallas_call(functools.partial(attn_kernel, n_cp, n_tp, heads, grp, hea...  115 us
    pallas_call x1, Pallas kernels, expert_layer(): pl.pallas_call(functools.partial(expert_kernel, n_chips, order, rounds),...  101 us

profile of v5, /device:TPU:0, one launch (start us, length us, event | category | flops | bytes accessed | tf_op | source)
XLA Modules:
  0.0 220.2 jit_solution(6738125920630151064)
XLA Ops:
  0.0 0.7 fusion.2
  0.7 0.2 fusion
  0.9 1.3 select_reduce_fusion
  2.3 114.6 %causal_attention.1 = (bf16[512,1024]{1,0:T(8,128)(2,1)}, bf16[1,1024,1792]{2,1,0:T(8,128)(2,1)}, bf16[1,1024,1792]{2,1,0:T(8,128)(2,1)}, bf16[1,1792,1024]{2,1,0:T(8,128)(2,1)}) custom-call(bf16[512,1024]{1,0:T(8,128)(2,1)} %x_ref.1, bf16[256,1024]{1,0:T(8,128)(2,1)} %bitcast.14, bf16[64,1024]{1,0:T(8,128)(2,1)} %bitcast.16, bf16[64,1024]{1,0:T(8,128)(2,1)} %bitcast.17, ...), custom_call_target="tpu_custom_call" | custom-call | flops 17179869184 | bytes 41943040 | tf_op jit(solution)/shard_map/causal_attention/pallas_call | solution.py:294
  116.9 100.6 %expert_layer.1 = f32[512,1024]{1,0:T(8,128)} custom-call(bf16[512,1024]{1,0:T(8,128)(2,1)} %get-tuple-element.9.h_ref, s32[2,512]{1,0:T(2,128)} %bitcast.13, f32[2,512]{1,0:T(2,128)} %bitcast.18, bf16[1,1024,1792]{2,1,0:T(8,128)(2,1)} %gate_a.1, bf16[1,1024,1792]{2,1,0:T(8,128)(2,1)} %get-tuple-element.10.gate_b, bf16[1,1024,1792]{2,1,0:T(8,128)(2,1)} %up_a.1, ...), custom_call_target="tpu_custom_call" | custom-call | flops 22548578304 | bytes 33554432 | tf_op jit(solution)/shard_map/expert_layer/pallas_call | solution.py:465
  217.5 2.7 %convert_element_type.14 = bf16[512,1024]{1,0:T(8,128)(2,1)} convert(f32[512,1024]{1,0:T(8,128)} %expert_layer.1) | non-fusion elementwise | flops 524288 | bytes 3145728 | tf_op jit(solution)/shard_map/convert_element_type | solution.py:519
  (1 shorter events, 0.0 us)

commit v6 on v5

--- a/solution.py
+++ b/solution.py
@@ -192,6 +192,7 @@
     project(pair, 0, blk)
     finish_half(my_half)
     run(2, lambda num: (2 * my_half + num, me * 4 + 2 * my_half + num), True)
+    run(1, lambda num: (2 * my_half + 1, me * 4 + 2 * my_half), False)
     for num in range(pieces):
         far_copies[num].wait_recv()
         pass_copies[num].start()
@@ -205,12 +206,12 @@
     run(2, lambda num: (2 * far_half + num, me * 4 + 2 * far_half + num), True)
 
     def place_local(num):
-        late = (num + 2) // 4
-        block = (1 - late) * (1 + 2 * num) + late * (1 + num // 2)
-        half = (1 - late) * num
-        return block, me * 4 + half * 2 + late * (num % 2)
-
-    run(6, place_local, False)
+        late = (num + 4) // 5
+        block = (1 - late) * (2 * far_half + 1) + late * (1 + (num + 1) // 2)
+        at = (1 - late) * 2 * far_half + late * ((num + 1) % 2)
+        return block, me * 4 + at
+
+    run(5, place_local, False)
 
     def visit_rank(turn, carry):
         step, part = turn // 2, turn % 2

time: 220 us -> 218 us (level)
  no operation moved by 1% of the time
where the time goes in v6:
time: 218 us
  Pallas kernels  213 us (98%)
  other arithmetic  4.75 us (2%)
    pallas_call x1, Pallas kernels, attention(): pl.pallas_call(functools.partial(attn_kernel, n_cp, n_tp, heads, grp, hea...  113 us
    pallas_call x1, Pallas kernels, expert_layer(): pl.pallas_call(functools.partial(expert_kernel, n_chips, order, rounds),...  101 us

profile of v6, /device:TPU:0, one launch (start us, length us, event | category | flops | bytes accessed | tf_op | source)
XLA Modules:
  0.0 218.2 jit_solution(16096247924190509491)
XLA Ops:
  0.0 0.7 fusion.2
  0.7 0.2 fusion
  0.9 1.3 select_reduce_fusion
  2.3 112.6 %causal_attention.1 = (bf16[512,1024]{1,0:T(8,128)(2,1)}, bf16[1,1024,1792]{2,1,0:T(8,128)(2,1)}, bf16[1,1024,1792]{2,1,0:T(8,128)(2,1)}, bf16[1,1792,1024]{2,1,0:T(8,128)(2,1)}) custom-call(bf16[512,1024]{1,0:T(8,128)(2,1)} %x_ref.1, bf16[256,1024]{1,0:T(8,128)(2,1)} %bitcast.14, bf16[64,1024]{1,0:T(8,128)(2,1)} %bitcast.16, bf16[64,1024]{1,0:T(8,128)(2,1)} %bitcast.17, ...), custom_call_target="tpu_custom_call" | custom-call | flops 17179869184 | bytes 41943040 | tf_op jit(solution)/shard_map/causal_attention/pallas_call | solution.py:295
  114.8 100.6 %expert_layer.1 = f32[512,1024]{1,0:T(8,128)} custom-call(bf16[512,1024]{1,0:T(8,128)(2,1)} %get-tuple-element.9.h_ref, s32[2,512]{1,0:T(2,128)} %bitcast.13, f32[2,512]{1,0:T(2,128)} %bitcast.18, bf16[1,1024,1792]{2,1,0:T(8,128)(2,1)} %gate_a.1, bf16[1,1024,1792]{2,1,0:T(8,128)(2,1)} %get-tuple-element.10.gate_b, bf16[1,1024,1792]{2,1,0:T(8,128)(2,1)} %up_a.1, ...), custom_call_target="tpu_custom_call" | custom-call | flops 22548578304 | bytes 33554432 | tf_op jit(solution)/shard_map/expert_layer/pallas_call | solution.py:466
  215.5 2.7 %convert_element_type.14 = bf16[512,1024]{1,0:T(8,128)(2,1)} convert(f32[512,1024]{1,0:T(8,128)} %expert_layer.1) | non-fusion elementwise | flops 524288 | bytes 3145728 | tf_op jit(solution)/shard_map/convert_element_type | solution.py:520
  (1 shorter events, 0.0 us)
